TPU v7x, 32 devices: a whole 2x2x4 slice. The times are simulated.
32 devices in a mesh: zero: 8 (over y, x, core), tp: 4 (over z).
Axes of the slice: x: 2, y: 2, z: 4, core: 2. Of those that a mesh axis runs over, the one named last changes fastest.
Arguments:
- weight_gate: bfloat16 [2560, 9728], P('zero', 'tp'), may hold values from -0.125 to 0.125
- low_gate: bfloat16 [2560, 16], P('zero'), may hold values from -0.125 to 0.125
- high_gate: bfloat16 [16, 9728], P(None, 'tp'), may hold values from -1.5 to 1.5
- weight_up: bfloat16 [2560, 9728], P('zero', 'tp'), may hold values from -0.125 to 0.125
- low_up: bfloat16 [2560, 16], P('zero'), may hold values from -0.125 to 0.125
- high_up: bfloat16 [16, 9728], P(None, 'tp'), may hold values from -1.5 to 1.5
- weight_down: bfloat16 [9728, 2560], P('tp', 'zero'), may hold values from -0.0625 to 0.0625
- low_down: bfloat16 [9728, 16], P('tp'), may hold values from -0.0625 to 0.0625
- high_down: bfloat16 [16, 2560], P(None, 'zero'), may hold values from -1.5 to 1.5
- norm_train: float32 [2560], P(('zero', 'tp')), may hold values from 0.25 to 1.75
- norm_step: float32 [2560], P(('zero', 'tp')), may hold values from -0.3 to 0.3
Outputs:
- ready_gate: bfloat16 [2560, 9728], P(None, 'tp')
- ready_up: bfloat16 [2560, 9728], P(None, 'tp')
- ready_down: bfloat16 [9728, 2560], P('tp')
- serve_norm: bfloat16 [2560], replicated
All inputs are finite; a program needn't handle non-finite values.
Results may differ from a plain program's by a relative error of at most 0.001.
Values may be sent and summed in bfloat16 or wider, within the bound.
A program may use at most 128 MiB of HBM per device.

v0:
```python
import functools

import jax
import jax.numpy as jnp
from jax import lax
from jax.experimental import pallas as pl
from jax.experimental.pallas import tpu as pltpu
from jax.sharding import PartitionSpec as P

mix_rate = 0.5
MESH = pl.DeviceIdType.MESH
LANES = 128
CHUNKS = 4
HALF = CHUNKS // 2
GROUP = 8
GRANT = 32 * 2**20
VMEM = pl.BlockSpec(memory_space=pltpu.VMEM)
ANY = pl.BlockSpec(memory_space=pl.ANY)
EARLY, LATE = range(HALF), range(HALF, CHUNKS)


def merge_rows(weight, factor, other):
    product = lax.dot_general(
        factor, other, (((0,), (0,)), ((), ())), preferred_element_type=jnp.float32
    )
    return (weight.astype(jnp.float32) + mix_rate * product).astype(jnp.bfloat16)


class Place:
    def __init__(self):
        me = lax.axis_index("zero")
        core = lax.rem(me, 2)
        x = lax.rem(lax.div(me, 2), 2)
        y = lax.div(me, 4)

        def at(yy, xx, cc):
            return (yy * 2 + xx) * 2 + cc

        self.me, self.core = me, core
        self.partner = at(y, x, 1 - core)
        self.across_x = at(y, 1 - x, core)
        self.across_y = at(1 - y, x, core)
        self.across = at(1 - y, 1 - x, core)
        self.group = [
            at(
                y + dy - 2 * y * dy,
                x + dx - 2 * x * dx,
                core + dc - 2 * core * dc,
            )
            for dy in (0, 1) for dx in (0, 1) for dc in (0, 1) if dy + dx + dc
        ]

    def other_core(self, owner):
        return owner + self.partner - self.me


def remote(src, dst, peer, send, recv):
    return pltpu.make_async_remote_copy(
        src_ref=src, dst_ref=dst, send_sem=send, recv_sem=recv,
        device_id={"zero": peer}, device_id_type=MESH,
    )


def first_kernel(
    tp,
    weight_down, factor_down, other_down,
    weight_gate, factor_gate, other_gate,
    weight_up, factor_up, other_up,
    norm_train, norm_step,
    gate, down, extra, gains, held, weights, w_sems,
    n_send, n_recv,
    x_send, x_recv, y_send, y_recv, fx_send, fx_recv, fy_send, fy_recv, p_send, p_recv,
    ex_send, ex_recv, ey_send, ey_recv,
):
    rows, columns = weight_gate.shape
    step = rows // CHUNKS
    z = Place()
    me = z.me

    loads = [
        pltpu.make_async_copy(weight, weights.at[i], w_sems.at[i])
        for i, weight in enumerate((weight_down, weight_gate, weight_up))
    ]
    for load in loads:
        load.start()

    mine = lax.axis_index("tp")
    peers, width = [{"zero": peer} for peer in z.group], 1
    while width < tp:
        bit = lax.rem(lax.div(mine, width), 2)
        peers.append({"tp": mine + width - 2 * width * bit})
        width *= 2

    barrier = pltpu.get_barrier_semaphore()
    for peer in peers:
        pl.semaphore_signal(barrier, inc=1, device_id=peer, device_id_type=MESH)
    place = mine * GROUP + me
    size = norm_train.shape[1]
    gains[place, :, 0:size] = norm_train[...] + norm_step[...]

    stacks = (held, gate)
    factors = (
        (factor_down, other_down), (factor_gate, other_gate), (factor_up, other_up)
    )

    def merge(i, c):
        factor, other = factors[i]
        first = c * step

        @pl.loop(0, columns // LANES)
        def _(t):
            cols = pl.ds(pl.multiple_of(t * LANES, LANES), LANES)
            block = merge_rows(
                weights[i, pl.ds(first, step), cols],
                factor[:, pl.ds(first, step)],
                other[:, cols],
            )
            if i < 2:
                stacks[i][pl.ds(pl.multiple_of(me * rows + first, 16), step), cols] = block
            else:
                extra[0, pl.ds(first, step), cols] = block

    loads[0].wait()
    merge(0, 0)
    pl.semaphore_wait(barrier, len(peers))

    def pass_gains(k, first, count):
        block = gains.at[pl.ds(first, count)]
        dma = pltpu.make_async_remote_copy(
            src_ref=block, dst_ref=block, send_sem=n_send.at[k], recv_sem=n_recv.at[k],
            device_id=peers[k], device_id_type=MESH,
        )
        dma.start()
        return dma

    def copy(i, owner, c, peer, send, recv):
        first = pl.multiple_of(owner * rows + c * step, 16)
        ref = stacks[i].at[pl.ds(first, step), :]
        return remote(ref, ref, peer, send, recv)

    def on_x(i, owner, c):
        return copy(i, owner, c, z.across_x, x_send.at[i, c], x_recv.at[i, c])

    def on_y(i, owner, c):
        return copy(i, owner, c, z.across_y, y_send.at[i, c], y_recv.at[i, c])

    def forward_x(i, owner, c):
        return copy(i, owner, c, z.across_x, fx_send.at[i, c - HALF], fx_recv.at[i, c - HALF])

    def forward_y(i, owner, c):
        return copy(i, owner, c, z.across_y, fy_send.at[i, c], fy_recv.at[i, c])

    def share(i, slot, owner, c):
        return copy(i, owner, c, z.partner, p_send.at[slot, i, c], p_recv.at[slot, i, c])

    def ahead_x(c):
        at = pl.ds(c * step, step)
        return remote(
            extra.at[0, at], extra.at[1, at], z.across_x, ex_send.at[c], ex_recv.at[c]
        )

    def ahead_y(c):
        at = pl.ds(c * step, step)
        return remote(
            extra.at[0, at], extra.at[2, at], z.across_y, ey_send.at[c], ey_recv.at[c]
        )

    sent = []

    def go(dma):
        dma.start()
        sent.append(dma)

    go(on_x(0, me, 0))
    passed = [pass_gains(k, place, 1) for k in range(len(z.group))]
    for i in range(2):
        if i:
            loads[i].wait()
        for c, d in zip(EARLY, LATE):
            if i or c:
                merge(i, c)
                go(on_x(i, me, c))
            merge(i, d)
            go(on_y(i, me, d))
        for c, d in zip(EARLY, LATE):
            go(on_x(i, me, d))
            go(on_y(i, me, c))
        for c in range(CHUNKS):
            go(share(i, 0, me, c))
    loads[2].wait()
    for c in range(CHUNKS):
        merge(2, c)

    for dma in passed:
        dma.wait_recv()
    for k in range(len(z.group), len(peers)):
        width = 1 << (k - len(z.group))
        passed.append(pass_gains(k, lax.div(mine, width) * (width * GROUP), width * GROUP))
        passed[-1].wait_recv()
    sent += passed

    def turn(owner):
        base = pl.multiple_of(lax.div(owner, 2) * (2 * rows), LANES)

        @pl.loop(0, columns // LANES)
        def _(t):
            cols = pl.ds(pl.multiple_of(t * LANES, LANES), LANES)
            down[cols, pl.ds(base, 2 * rows)] = held[pl.ds(base, 2 * rows), cols].T

    def shared(i, slot, owner):
        for c in range(CHUNKS):
            share(i, slot, z.other_core(owner), c).wait_recv()

    for i in range(2):
        for c, d in zip(EARLY, LATE):
            on_x(i, z.across_x, c).wait_recv()
            go(forward_y(i, z.across_x, c))
            go(share(i, 1, z.across_x, c))
            on_y(i, z.across_y, d).wait_recv()
            go(forward_x(i, z.across_y, d))
            go(share(i, 2, z.across_y, d))
        if i == 1:
            @pl.when(z.core == 1)
            def _():
                for c, d in zip(EARLY, LATE):
                    ahead_x(c).start()
                    ahead_y(d).start()
                for c, d in zip(EARLY, LATE):
                    ahead_x(d).start()
                    ahead_y(c).start()
        for c, d in zip(EARLY, LATE):
            on_x(i, z.across_x, d).wait_recv()
            go(share(i, 1, z.across_x, d))
            on_y(i, z.across_y, c).wait_recv()
            go(share(i, 2, z.across_y, c))
        for slot, owner in ((0, me), (1, z.across_x), (2, z.across_y)):
            shared(i, slot, owner)
            if i == 0:
                turn(owner)
    for i in range(2):
        for c, d in zip(EARLY, LATE):
            forward_y(i, z.across, c).wait_recv()
            go(share(i, 3, z.across, c))
            forward_x(i, z.across, d).wait_recv()
            go(share(i, 3, z.across, d))
        if i == 0:
            shared(i, 3, z.across)
            turn(z.across)
    shared(1, 3, z.across)
    for dma in sent:
        dma.wait_send()

    @pl.when(z.core == 1)
    def _():
        for c in range(CHUNKS):
            ahead_x(c).wait()
            ahead_y(c).wait()


def first(sources, norms, tp):
    rows, columns = sources[0].shape
    stack = (rows * GROUP, columns)
    turned = (columns, rows * GROUP)
    dma = pltpu.SemaphoreType.DMA
    stages = GROUP - 1 + tp.bit_length() - 1
    return pl.pallas_call(
        functools.partial(first_kernel, tp),
        out_shape=(
            pltpu.VMEM(stack, jnp.bfloat16),
            pltpu.VMEM(turned, jnp.bfloat16),
            pltpu.VMEM((3, rows, columns), jnp.bfloat16),
            pltpu.VMEM((GROUP * tp, 1, LANES), jnp.float32),
        ),
        in_specs=[ANY, VMEM, VMEM] * 3 + [VMEM, VMEM],
        out_specs=[VMEM] * 4,
        scratch_shapes=[
            pltpu.VMEM(stack, jnp.bfloat16),
            pltpu.VMEM((3, rows, columns), jnp.bfloat16),
            dma((3,)),
            dma((stages,)), dma((stages,)),
            dma((2, CHUNKS)), dma((2, CHUNKS)), dma((2, CHUNKS)), dma((2, CHUNKS)),
            dma((2, HALF)), dma((2, HALF)), dma((2, HALF)), dma((2, HALF)),
            dma((4, 2, CHUNKS)), dma((4, 2, CHUNKS)),
            dma((CHUNKS,)), dma((CHUNKS,)), dma((CHUNKS,)), dma((CHUNKS,)),
        ],
        compiler_params=pltpu.CompilerParams(
            collective_id=0, has_side_effects=True, vmem_limit_bytes=GRANT
        ),
        name="gather_first",
    )(*sources, *norms)


def second_kernel(
    extra, after, up, ready, l_sems,
    x_send, x_recv, y_send, y_recv, fx_send, fx_recv, fy_send, fy_recv, p_send, p_recv,
):
    _, rows, columns = extra.shape
    step = rows // CHUNKS
    z = Place()
    me = z.me

    barrier = pltpu.get_barrier_semaphore()
    for peer in (z.across_x, z.across_y):
        pl.semaphore_signal(barrier, inc=1, device_id={"zero": peer}, device_id_type=MESH)

    @pl.when(z.core == 0)
    def _():
        pl.semaphore_signal(
            barrier, inc=1, device_id={"zero": z.partner}, device_id_type=MESH
        )

    pl.semaphore_wait(barrier, 2 + z.core)

    def part(owner, c):
        return up.at[pl.ds(pl.multiple_of(owner * rows + c * step, 16), step), :]

    def kept(slot, c):
        return extra.at[slot, pl.ds(c * step, step)]

    def on_x(c):
        return remote(kept(0, c), part(me, c), z.across_x, x_send.at[c], x_recv.at[c])

    def on_y(c):
        return remote(kept(0, c), part(me, c), z.across_y, y_send.at[c], y_recv.at[c])

    def forward_x(src, c):
        return remote(
            src, part(z.across_y, c), z.across_x, fx_send.at[c - HALF], fx_recv.at[c - HALF]
        )

    def forward_y(src, c):
        return remote(src, part(z.across_x, c), z.across_y, fy_send.at[c], fy_recv.at[c])

    def share(src, slot, owner, c):
        return remote(src, part(owner, c), z.partner, p_send.at[slot, c], p_recv.at[slot, c])

    def move(slot, owner):
        at = pl.ds(pl.multiple_of(owner * rows, 16), rows)
        return pltpu.make_async_copy(extra.at[slot], up.at[at, :], l_sems.at[slot])

    owners = (me, z.across_x, z.across_y)

    @pl.when(z.core == 0)
    def _():
        for c, d in zip(EARLY, LATE):
            on_x(c).start()
            on_y(d).start()
        for c, d in zip(EARLY, LATE):
            on_x(d).start()
            on_y(c).start()
        move(0, me).start()
        for c, d in zip(EARLY, LATE):
            on_x(c).wait_recv()
            forward_y(part(z.across_x, c), c).start()
            on_y(d).wait_recv()
            forward_x(part(z.across_y, d), d).start()
        for c, d in zip(EARLY, LATE):
            on_x(d).wait_recv()
            on_y(c).wait_recv()
        pl.semaphore_wait(ready, 1)
        for c in range(CHUNKS):
            share(kept(0, c), 0, me, c).start()
        for slot in (1, 2):
            for c in range(CHUNKS):
                share(part(owners[slot], c), slot, owners[slot], c).start()
        for c in range(CHUNKS):
            on_x(c).wait_send()
            on_y(c).wait_send()
        move(0, me).wait()

    @pl.when(z.core == 1)
    def _():
        pl.semaphore_signal(
            ready, inc=1, device_id={"zero": z.partner}, device_id_type=MESH
        )
        for c, d in zip(EARLY, LATE):
            forward_y(kept(1, c), c).start()
            forward_x(kept(2, d), d).start()
        for slot, owner in enumerate(owners):
            for c in range(CHUNKS):
                share(kept(slot, c), slot, owner, c).start()
        for slot, owner in enumerate(owners):
            move(slot, owner).start()
        for slot, owner in enumerate(owners):
            move(slot, owner).wait()

    for c, d in zip(EARLY, LATE):
        forward_y(kept(1, c), c).wait_recv()
        share(part(z.across, c), 3, z.across, c).start()
        forward_x(kept(2, d), d).wait_recv()
        share(part(z.across, d), 3, z.across, d).start()
    for slot, owner in enumerate((*owners, z.across)):
        for c in range(CHUNKS):
            share(part(owner, c), slot, z.other_core(owner), c).wait()
    for c, d in zip(EARLY, LATE):
        forward_y(kept(1, c), c).wait_send()
        forward_x(kept(2, d), d).wait_send()


def second(extra, after):
    _, rows, columns = extra.shape
    dma = pltpu.SemaphoreType.DMA
    extra = pltpu.with_memory_space_constraint(extra, pltpu.VMEM)
    return pl.pallas_call(
        second_kernel,
        out_shape=pltpu.VMEM((rows * GROUP, columns), jnp.bfloat16),
        in_specs=[VMEM, ANY],
        out_specs=VMEM,
        scratch_shapes=[
            pltpu.SemaphoreType.REGULAR,
            dma((3,)),
            dma((CHUNKS,)), dma((CHUNKS,)), dma((CHUNKS,)), dma((CHUNKS,)),
            dma((HALF,)), dma((HALF,)), dma((HALF,)), dma((HALF,)),
            dma((4, CHUNKS)), dma((4, CHUNKS)),
        ],
        compiler_params=pltpu.CompilerParams(
            collective_id=1, has_side_effects=True, vmem_limit_bytes=2**20
        ),
        name="gather_second",
    )(extra, after)


def start_stores(sources, targets, sems):
    pieces = 4
    copies = []
    for i, (src, dst) in enumerate(zip(sources, targets)):
        size = src.shape[0] // pieces
        for k in range(pieces):
            at = pl.ds(k * size, size)
            copies.append(pltpu.make_async_copy(src.at[at], dst.at[at], sems.at[i, k]))
            copies[-1].start()
    return copies


def store_kernel(count, *refs):
    for copy in start_stores(refs[:count], refs[count:-1], refs[-1]):
        copy.wait()


def store_norm_kernel(tp, size, gate, down, gains, gate_out, down_out, norm, lines, sems):
    copies = start_stores((gate, down), (gate_out, down_out), sems)
    lane = lax.broadcasted_iota(jnp.int32, (1, LANES), 1)
    parts = [[] for _ in range(lines.shape[0])]
    for k in range(GROUP * tp):
        zero, z = divmod(k, tp)
        piece = jnp.where(lane < size, gains[z * GROUP + zero], 0.0)
        line, shift = divmod(k * size, LANES)
        piece = pltpu.roll(piece, shift, 1) if shift else piece
        parts[line].append(jnp.where(lane >= shift, piece, 0.0))
        if shift + size > LANES:
            parts[line + 1].append(jnp.where(lane < shift, piece, 0.0))
    for line, terms in enumerate(parts):
        lines[pl.ds(line, 1), :] = sum(terms[1:], terms[0])
    norm[...] = lines[...].astype(jnp.bfloat16)
    for copy in copies:
        copy.wait()


def in_vmem(*arrays):
    return [pltpu.with_memory_space_constraint(a, pltpu.VMEM) for a in arrays]


def store(*held):
    held = in_vmem(*held)
    return pl.pallas_call(
        functools.partial(store_kernel, len(held)),
        out_shape=tuple(jax.ShapeDtypeStruct(a.shape, a.dtype) for a in held),
        in_specs=[VMEM] * len(held),
        out_specs=[ANY] * len(held),
        scratch_shapes=[pltpu.SemaphoreType.DMA((len(held), 4))],
        compiler_params=pltpu.CompilerParams(vmem_limit_bytes=2**20),
        name="store_merged",
    )(*held)


def store_norm(gate, down, gains, tp, size):
    held = in_vmem(gate, down, gains)
    lines = (GROUP * tp * size // LANES, LANES)
    shapes = [jax.ShapeDtypeStruct(a.shape, a.dtype) for a in held[:2]]
    return pl.pallas_call(
        functools.partial(store_norm_kernel, tp, size),
        out_shape=(*shapes, jax.ShapeDtypeStruct(lines, jnp.bfloat16)),
        in_specs=[VMEM] * 3,
        out_specs=[ANY, ANY, VMEM],
        scratch_shapes=[pltpu.VMEM(lines, jnp.float32), pltpu.SemaphoreType.DMA((2, 4))],
        compiler_params=pltpu.CompilerParams(vmem_limit_bytes=2**20),
        name="store_first",
    )(*held)


def local(
    weight_gate, low_gate, high_gate,
    weight_up, low_up, high_up,
    weight_down, low_down, high_down,
    norm_train, norm_step,
    *, fast, tp,
):
    sources = (
        (weight_down.T, high_down, low_down.T),
        (weight_gate, low_gate.T, high_gate),
        (weight_up, low_up.T, high_up),
    )
    if fast:
        norms = (norm_train[None], norm_step[None])
        gate, down, extra, gains = first(sum(sources, ()), norms, tp)
        ready_gate, ready_down, norm = store_norm(gate, down, gains, tp, norm_train.shape[0])
        (ready_up,) = store(second(extra, norm))
        serve_norm = norm.reshape(-1)
    else:
        down, gate, up = (merge_rows(*s) for s in sources)
        ready_gate, ready_up, ready_down = (
            lax.all_gather(a, "zero", axis=0, tiled=True) for a in (gate, up, down)
        )
        ready_down = ready_down.T
        serve_norm = lax.all_gather(
            (norm_train + norm_step).astype(jnp.bfloat16), ("zero", "tp"), axis=0, tiled=True
        )
    return (ready_gate, ready_up, ready_down, serve_norm)


def solution(mesh):
    def step(*args):
        zero, tp = mesh.shape["zero"], mesh.shape["tp"]
        rows, columns = args[0].shape[0] // zero, args[0].shape[1] // tp
        fast = (
            zero == GROUP
            and tp & (tp - 1) == 0
            and args[9].shape[0] <= zero * tp * LANES
            and args[9].shape[0] % LANES == 0
            and rows % (16 * CHUNKS) == 0
            and columns % LANES == 0
            and 2 * rows % LANES == 0
            and args[6].shape == args[0].shape[::-1]
        )
        return jax.shard_map(
            functools.partial(local, fast=fast, tp=tp),
            mesh=mesh,
            in_specs=(
                P("zero", "tp"), P("zero", None), P(None, "tp"),
                P("zero", "tp"), P("zero", None), P(None, "tp"),
                P("tp", "zero"), P("tp", None), P(None, "zero"),
                P(("zero", "tp")), P(("zero", "tp")),
            ),
            out_specs=(P(None, "tp"), P(None, "tp"), P("tp", None), P()),
            check_vma=False,
        )(*args)

    return step
```

profile of v0, /device:TPU:0, one launch (start us, length us, event | category | flops | bytes accessed | tf_op | source)
XLA Modules:
  0.0 174.2 jit_solution(11301606808754566594)
XLA Ops:
  0.6 119.8 %gather_first.1 = (bf16[2560,2432]{1,0:T(8,128)(2,1)S(1)}, bf16[2432,2560]{1,0:T(8,128)(2,1)S(1)}, bf16[3,320,2432]{2,1,0:T(8,128)(2,1)S(1)}, f32[32,1,128]{2,1,0:T(1,128)S(1)}) custom-call(bf16[320,2432]{1,0:T(8,128)(2,1)} %bitcast.8, bf16[16,320]{1,0:T(8,128)(2,1)} %factor_down.1, bf16[16,2432]{1,0:T(8,128)(2,1)} %bitcast.9, ...), custom_call_target="tpu_custom_call" | custom-call | tf_op jit(solution)/shard_map/gather_first/pallas_call | solution.py:266
  120.4 9.1 %store_first.1 = (bf16[2560,2432]{1,0:T(8,128)(2,1)}, bf16[2432,2560]{1,0:T(8,128)(2,1)}, bf16[20,128]{1,0:T(8,128)(2,1)}) custom-call(bf16[2560,2432]{1,0:T(8,128)(2,1)S(1)} %get-tuple-element.11.gate, bf16[2432,2560]{1,0:T(8,128)(2,1)S(1)} %get-tuple-element.12.down, f32[32,1,128]{2,1,0:T(1,128)S(1)} %get-tuple-element.13.gains), custom_call_target="tpu_custom_call" | custom-call | tf_op jit(solution)/shard_map/store_first/pallas_call | solution.py:480
  129.5 0.0 copy-start
  129.5 0.7 copy-done
  130.2 39.4 %gather_second.1.refs_0_ = bf16[2560,2432]{1,0:T(8,128)(2,1)S(1)} custom-call(bf16[3,320,2432]{2,1,0:T(8,128)(2,1)S(1)} %get-tuple-element.15.extra, bf16[20,128]{1,0:T(8,128)(2,1)S(1)} %copy-done), custom_call_target="tpu_custom_call" | custom-call | tf_op jit(solution)/shard_map/gather_second/pallas_call | solution.py:404
  169.5 4.7 %store_merged.1 = bf16[2560,2432]{1,0:T(8,128)(2,1)} custom-call(bf16[2560,2432]{1,0:T(8,128)(2,1)S(1)} %gather_second.1.refs_0_), custom_call_target="tpu_custom_call" | custom-call | tf_op jit(solution)/shard_map/store_merged/pallas_call | solution.py:465
Async XLA Ops:
  129.5 0.7 copy-start
where the time goes:
time: 174 us
  Pallas kernels  173 us (99%)
    pallas_call x1, Pallas kernels, first(): pl.pallas_call(functools.partial(first_kernel, tp), out_shape=(pltpu.VMEM...  120 us
    pallas_call x1, Pallas kernels, second(): pl.pallas_call(second_kernel, out_shape=pltpu.VMEM((rows * GROUP, columns...  39.4 us
    pallas_call x1, Pallas kernels, store_norm(): pl.pallas_call(functools.partial(store_norm_kernel, tp, size), out_shape=...  9.06 us
    pallas_call x1, Pallas kernels, store(): pl.pallas_call(functools.partial(store_kernel, len(held)), out_shape=tupl...  4.67 us

commit v1 on v0

--- a/solution.py
+++ b/solution.py
@@ -10,6 +10,7 @@
 mix_rate = 0.5
 MESH = pl.DeviceIdType.MESH
 LANES = 128
+TILE = 2 * LANES
 CHUNKS = 4
 HALF = CHUNKS // 2
 GROUP = 8
@@ -17,13 +18,18 @@
 VMEM = pl.BlockSpec(memory_space=pltpu.VMEM)
 ANY = pl.BlockSpec(memory_space=pl.ANY)
 EARLY, LATE = range(HALF), range(HALF, CHUNKS)
+FIRST = [c for pair in zip(EARLY, LATE) for c in pair]
+
+
+def merged(weight, product):
+    return (weight.astype(jnp.float32) + mix_rate * product).astype(jnp.bfloat16)
 
 
 def merge_rows(weight, factor, other):
     product = lax.dot_general(
         factor, other, (((0,), (0,)), ((), ())), preferred_element_type=jnp.float32
     )
-    return (weight.astype(jnp.float32) + mix_rate * product).astype(jnp.bfloat16)
+    return merged(weight, product)
 
 
 class Place:
@@ -67,7 +73,7 @@
     weight_gate, factor_gate, other_gate,
     weight_up, factor_up, other_up,
     norm_train, norm_step,
-    gate, down, extra, gains, held, weights, w_sems,
+    gate, down, extra, gains, held, weights, lefts, rights, norms, w_sems,
     n_send, n_recv,
     x_send, x_recv, y_send, y_recv, fx_send, fx_recv, fy_send, fy_recv, p_send, p_recv,
     ex_send, ex_recv, ey_send, ey_recv,
@@ -77,13 +83,6 @@
     z = Place()
     me = z.me
 
-    loads = [
-        pltpu.make_async_copy(weight, weights.at[i], w_sems.at[i])
-        for i, weight in enumerate((weight_down, weight_gate, weight_up))
-    ]
-    for load in loads:
-        load.start()
-
     mine = lax.axis_index("tp")
     peers, width = [{"zero": peer} for peer in z.group], 1
     while width < tp:
@@ -94,34 +93,54 @@
     barrier = pltpu.get_barrier_semaphore()
     for peer in peers:
         pl.semaphore_signal(barrier, inc=1, device_id=peer, device_id_type=MESH)
-    place = mine * GROUP + me
-    size = norm_train.shape[1]
-    gains[place, :, 0:size] = norm_train[...] + norm_step[...]
+
+    loads = []
+
+    def load(src, dst):
+        loads.append(pltpu.make_async_copy(src, dst, w_sems.at[len(loads)]))
+        loads[-1].start()
+        return loads[-1]
+
+    wide = ((weight_down, factor_down, other_down), (weight_gate, factor_gate, other_gate),
+            (weight_up, factor_up, other_up))
+    narrow = [[load(factor, lefts.at[0]), load(other, rights.at[0])]
+              for _, factor, other in wide[:1]]
+    pieces = [[load(wide[0][0].at[pl.ds(c * step, step)], weights.at[0, pl.ds(c * step, step)])
+               for c in FIRST]]
+    norm_loads = [load(norm_train, norms.at[0]), load(norm_step, norms.at[1])]
+    for i in (1, 2):
+        weight, factor, other = wide[i]
+        narrow.append([load(factor, lefts.at[i]), load(other, rights.at[i])])
+        pieces.append([load(weight, weights.at[i])])
 
     stacks = (held, gate)
-    factors = (
-        (factor_down, other_down), (factor_gate, other_gate), (factor_up, other_up)
-    )
+
+    turned = [None] * 3
 
     def merge(i, c):
-        factor, other = factors[i]
-        first = c * step
-
-        @pl.loop(0, columns // LANES)
-        def _(t):
-            cols = pl.ds(pl.multiple_of(t * LANES, LANES), LANES)
-            block = merge_rows(
-                weights[i, pl.ds(first, step), cols],
-                factor[:, pl.ds(first, step)],
-                other[:, cols],
-            )
+        other = rights.at[i]
+        if turned[i] is None:
+            for dma in narrow[i]:
+                dma.wait()
+            turned[i] = lefts[i].T
+        if i == 0:
+            pieces[0][FIRST.index(c)].wait()
+        elif c == 0:
+            pieces[i][0].wait()
+        lhs = turned[i][c * step:(c + 1) * step]
+        here = pl.ds(c * step, step)
+        for t in range(0, columns, TILE):
+            cols = pl.ds(t, min(TILE, columns - t))
+            product = jnp.dot(lhs, other[:, cols], preferred_element_type=jnp.float32)
+            block = merged(weights[i, here, cols], product)
             if i < 2:
-                stacks[i][pl.ds(pl.multiple_of(me * rows + first, 16), step), cols] = block
+                own = pl.ds(pl.multiple_of(me * rows + c * step, 16), step)
+                stacks[i][own, cols] = block
             else:
-                extra[0, pl.ds(first, step), cols] = block
-
-    loads[0].wait()
+                extra[0, here, cols] = block
+
     merge(0, 0)
+    merge(0, HALF)
     pl.semaphore_wait(barrier, len(peers))
 
     def pass_gains(k, first, count):
@@ -172,22 +191,25 @@
         sent.append(dma)
 
     go(on_x(0, me, 0))
+    go(on_y(0, me, HALF))
+    place = mine * GROUP + me
+    for dma in norm_loads:
+        dma.wait()
+    size = norm_train.shape[1]
+    gains[place, :, 0:size] = norms[0] + norms[1]
     passed = [pass_gains(k, place, 1) for k in range(len(z.group))]
     for i in range(2):
-        if i:
-            loads[i].wait()
         for c, d in zip(EARLY, LATE):
             if i or c:
                 merge(i, c)
                 go(on_x(i, me, c))
-            merge(i, d)
-            go(on_y(i, me, d))
+                merge(i, d)
+                go(on_y(i, me, d))
         for c, d in zip(EARLY, LATE):
             go(on_x(i, me, d))
             go(on_y(i, me, c))
         for c in range(CHUNKS):
             go(share(i, 0, me, c))
-    loads[2].wait()
     for c in range(CHUNKS):
         merge(2, c)
 
@@ -271,12 +293,15 @@
             pltpu.VMEM((3, rows, columns), jnp.bfloat16),
             pltpu.VMEM((GROUP * tp, 1, LANES), jnp.float32),
         ),
-        in_specs=[ANY, VMEM, VMEM] * 3 + [VMEM, VMEM],
+        in_specs=[ANY] * 11,
         out_specs=[VMEM] * 4,
         scratch_shapes=[
             pltpu.VMEM(stack, jnp.bfloat16),
             pltpu.VMEM((3, rows, columns), jnp.bfloat16),
-            dma((3,)),
+            pltpu.VMEM((3, *sources[1].shape), jnp.bfloat16),
+            pltpu.VMEM((3, *sources[2].shape), jnp.bfloat16),
+            pltpu.VMEM((2, *norms[0].shape), jnp.float32),
+            dma((CHUNKS + 10,)),
             dma((stages,)), dma((stages,)),
             dma((2, CHUNKS)), dma((2, CHUNKS)), dma((2, CHUNKS)), dma((2, CHUNKS)),
             dma((2, HALF)), dma((2, HALF)), dma((2, HALF)), dma((2, HALF)),

time: 174 us -> 165 us (0.948)
  Pallas kernels: 173 us -> 164 us
    pallas_call x1, Pallas kernels: 120 us -> 111 us  [first(): pl.pallas_call(functools.partial(first_kernel, tp), out_shape=(pltpu.VMEM...]
where the time goes in v1:
time: 165 us
  Pallas kernels  164 us (99%)
    pallas_call x1, Pallas kernels, first(): pl.pallas_call(functools.partial(first_kernel, tp), out_shape=(pltpu.VMEM...  111 us
    pallas_call x1, Pallas kernels, second(): pl.pallas_call(second_kernel, out_shape=pltpu.VMEM((rows * GROUP, columns...  39.4 us
    pallas_call x1, Pallas kernels, store_norm(): pl.pallas_call(functools.partial(store_norm_kernel, tp, size), out_shape=...  9.06 us
    pallas_call x1, Pallas kernels, store(): pl.pallas_call(functools.partial(store_kernel, len(held)), out_shape=tupl...  4.67 us

profile of v1, /device:TPU:0, one launch (start us, length us, event | category | flops | bytes accessed | tf_op | source)
XLA Modules:
  0.0 165.1 jit_solution(5019931456004832351)
XLA Ops:
  0.6 110.7 %gather_first.1 = (bf16[2560,2432]{1,0:T(8,128)(2,1)S(1)}, bf16[2432,2560]{1,0:T(8,128)(2,1)S(1)}, bf16[3,320,2432]{2,1,0:T(8,128)(2,1)S(1)}, f32[32,1,128]{2,1,0:T(1,128)S(1)}) custom-call(bf16[320,2432]{1,0:T(8,128)(2,1)} %bitcast.8, bf16[16,320]{1,0:T(8,128)(2,1)} %factor_down.1, bf16[16,2432]{1,0:T(8,128)(2,1)} %bitcast.9, ...), custom_call_target="tpu_custom_call" | custom-call | tf_op jit(solution)/shard_map/gather_first/pallas_call | solution.py:288
  111.3 9.1 %store_first.1 = (bf16[2560,2432]{1,0:T(8,128)(2,1)}, bf16[2432,2560]{1,0:T(8,128)(2,1)}, bf16[20,128]{1,0:T(8,128)(2,1)}) custom-call(bf16[2560,2432]{1,0:T(8,128)(2,1)S(1)} %get-tuple-element.11.gate, bf16[2432,2560]{1,0:T(8,128)(2,1)S(1)} %get-tuple-element.12.down, f32[32,1,128]{2,1,0:T(1,128)S(1)} %get-tuple-element.13.gains), custom_call_target="tpu_custom_call" | custom-call | tf_op jit(solution)/shard_map/store_first/pallas_call | solution.py:505
  120.4 0.0 copy-start
  120.4 0.7 copy-done
  121.1 39.4 %gather_second.1.refs_0_ = bf16[2560,2432]{1,0:T(8,128)(2,1)S(1)} custom-call(bf16[3,320,2432]{2,1,0:T(8,128)(2,1)S(1)} %get-tuple-element.15.extra, bf16[20,128]{1,0:T(8,128)(2,1)S(1)} %copy-done), custom_call_target="tpu_custom_call" | custom-call | tf_op jit(solution)/shard_map/gather_second/pallas_call | solution.py:429
  160.4 4.7 %store_merged.1 = bf16[2560,2432]{1,0:T(8,128)(2,1)} custom-call(bf16[2560,2432]{1,0:T(8,128)(2,1)S(1)} %gather_second.1.refs_0_), custom_call_target="tpu_custom_call" | custom-call | tf_op jit(solution)/shard_map/store_merged/pallas_call | solution.py:490
Async XLA Ops:
  120.4 0.7 copy-start

commit v2 on v1

v2 whole, which is shorter than its diff:
```python
import functools

import jax
import jax.numpy as jnp
from jax import lax
from jax.experimental import pallas as pl
from jax.experimental.pallas import tpu as pltpu
from jax.sharding import PartitionSpec as P

mix_rate = 0.5
MESH = pl.DeviceIdType.MESH
LANES = 128
TILE = 2 * LANES
GROUP = 8
CHUNKS = 4
STAGES = (8, 8, 4)
COUNTS = (4, 4, 4)
PASSED = (0, 1, 2)
GRANT = 32 * 2**20
VMEM = pl.BlockSpec(memory_space=pltpu.VMEM)
ANY = pl.BlockSpec(memory_space=pl.ANY)


def merged(weight, product):
    return (weight.astype(jnp.float32) + mix_rate * product).astype(jnp.bfloat16)


def merge_rows(weight, factor, other):
    product = lax.dot_general(
        factor, other, (((0,), (0,)), ((), ())), preferred_element_type=jnp.float32
    )
    return merged(weight, product)


def stage_rows(rows):
    return [2 * rows * share // sum(STAGES) for share in STAGES]


class Place:
    def __init__(self):
        me = lax.axis_index("zero")
        core = lax.rem(me, 2)
        x = lax.rem(lax.div(me, 2), 2)
        y = lax.div(me, 4)

        def at(yy, xx, cc):
            return (yy * 2 + xx) * 2 + cc

        self.me, self.core = me, core
        self.partner = at(y, x, 1 - core)
        self.across_x = at(y, 1 - x, core)
        self.across_y = at(1 - y, x, core)
        self.across = at(1 - y, 1 - x, core)
        self.group = [
            at(
                y + dy - 2 * y * dy,
                x + dx - 2 * x * dx,
                core + dc - 2 * core * dc,
            )
            for dy in (0, 1) for dx in (0, 1) for dc in (0, 1) if dy + dx + dc
        ]

    def other_core(self, owner):
        return owner + self.partner - self.me


def remote(src, dst, peer, send, recv):
    return pltpu.make_async_remote_copy(
        src_ref=src, dst_ref=dst, send_sem=send, recv_sem=recv,
        device_id={"zero": peer}, device_id_type=MESH,
    )


class Stack:
    def __init__(self, z, part, count, sems):
        self.z, self.part, self.count, self.half = z, part, count, count // 2
        (self.x_send, self.x_recv, self.y_send, self.y_recv,
         self.fx_send, self.fx_recv, self.fy_send, self.fy_recv,
         self.p_send, self.p_recv) = sems
        self.pairs = list(zip(range(self.half), range(self.half, count)))

    @staticmethod
    def sems(count):
        dma = pltpu.SemaphoreType.DMA
        return [dma((count,))] * 4 + [dma((count // 2,))] * 4 + [dma((4, count))] * 2

    def copy(self, owner, c, peer, send, recv, src=None):
        ref = self.part(owner, c)
        return remote(ref if src is None else src, ref, peer, send, recv)

    def on_x(self, c, src=None):
        z = self.z
        return self.copy(z.me, c, z.across_x, self.x_send.at[c], self.x_recv.at[c], src)

    def on_y(self, c, src=None):
        z = self.z
        return self.copy(z.me, c, z.across_y, self.y_send.at[c], self.y_recv.at[c], src)

    def forward_x(self, c, src=None):
        z, k = self.z, c - self.half
        return self.copy(z.across_y, c, z.across_x, self.fx_send.at[k], self.fx_recv.at[k], src)

    def forward_y(self, c, src=None):
        z = self.z
        return self.copy(z.across_x, c, z.across_y, self.fy_send.at[c], self.fy_recv.at[c], src)

    def share(self, slot, owner, c, src=None):
        return self.copy(
            owner, c, self.z.partner, self.p_send.at[slot, c], self.p_recv.at[slot, c], src
        )

    def shared(self, slot, owner):
        for c in range(self.count):
            self.share(slot, owner, c).wait_recv()


class Ahead:
    def __init__(self, z, own, landed, s, sems):
        self.z, self.own, self.landed = z, own, landed
        self.count, self.step = COUNTS[s], own.shape[0] // COUNTS[s]
        (self.x_send, self.x_recv, self.y_send, self.y_recv,
         self.fx_send, self.fx_recv, self.fy_send, self.fy_recv) = sems
        self.pairs = list(zip(range(self.count // 2), range(self.count // 2, self.count)))
        self.passed = list(enumerate(self.pairs[:PASSED[s]]))

    @staticmethod
    def sems(s):
        dma = pltpu.SemaphoreType.DMA
        return [dma((COUNTS[s],))] * 4 + [dma((max(PASSED[s], 1),))] * 4

    def at(self, c):
        return pl.ds(c * self.step, self.step)

    def on_x(self, c):
        return remote(
            self.own.at[self.at(c)], self.landed.at[0, self.at(c)], self.z.across_x,
            self.x_send.at[c], self.x_recv.at[c],
        )

    def on_y(self, c):
        return remote(
            self.own.at[self.at(c)], self.landed.at[1, self.at(c)], self.z.across_y,
            self.y_send.at[c], self.y_recv.at[c],
        )

    def pass_y(self, k, c):
        return remote(
            self.landed.at[0, self.at(c)], self.landed.at[2, self.at(c)], self.z.across_y,
            self.fy_send.at[k], self.fy_recv.at[k],
        )

    def pass_x(self, k, d):
        return remote(
            self.landed.at[1, self.at(d)], self.landed.at[2, self.at(d)], self.z.across_x,
            self.fx_send.at[k], self.fx_recv.at[k],
        )

    def start(self):
        for c, d in self.pairs:
            self.on_x(c).start()
            self.on_y(d).start()
        for c, d in self.pairs:
            self.on_x(d).start()
            self.on_y(c).start()

    def finish(self):
        for k, (c, d) in self.passed:
            self.on_x(c).wait_recv()
            self.pass_y(k, c).start()
            self.on_y(d).wait_recv()
            self.pass_x(k, d).start()
        early = [c for _, (c, _) in self.passed]
        late = [d for _, (_, d) in self.passed]
        for c in range(self.count):
            self.on_x(c).wait_send()
            self.on_y(c).wait_send()
            if c not in early:
                self.on_x(c).wait_recv()
            if c not in late:
                self.on_y(c).wait_recv()
        for k, (c, d) in self.passed:
            self.pass_y(k, c).wait()
            self.pass_x(k, d).wait()


def first_kernel(tp, *refs):
    refs = list(refs)

    def take(count):
        taken, refs[:] = refs[:count], refs[count:]
        return taken

    kept = len(STAGES) - 1
    sources = [take(3) for _ in range(3)]
    norm_train, norm_step = take(2)
    block, down = take(2)
    owns = take(kept)
    landed, gains = take(2)
    held, weights, lefts, rights, norms, w_sems, n_send, n_recv = take(8)
    rows, columns = sources[1][0].shape
    step = rows // CHUNKS
    z = Place()
    me = z.me
    spans = stage_rows(rows)
    step_1 = spans[0] // COUNTS[0]

    def held_part(owner, c):
        return held.at[pl.ds(pl.multiple_of(owner * rows + c * step, 16), step), :]

    def block_part(owner, c):
        return block.at[owner, pl.ds(c * step_1, step_1)]

    stacks = (
        Stack(z, held_part, CHUNKS, take(10)), Stack(z, block_part, COUNTS[0], take(10))
    )
    ahead = Ahead(z, owns[0], landed, 1, take(8))

    mine = lax.axis_index("tp")
    peers, width = [{"zero": peer} for peer in z.group], 1
    while width < tp:
        bit = lax.rem(lax.div(mine, width), 2)
        peers.append({"tp": mine + width - 2 * width * bit})
        width *= 2

    barrier = pltpu.get_barrier_semaphore()
    for peer in peers:
        pl.semaphore_signal(barrier, inc=1, device_id=peer, device_id_type=MESH)

    loads = []

    def load(src, dst):
        loads.append(pltpu.make_async_copy(src, dst, w_sems.at[len(loads)]))
        loads[-1].start()
        return loads[-1]

    def load_narrow(i):
        _, factor, other = sources[i]
        return [load(factor, lefts.at[i]), load(other, rights.at[i])]

    order = [c for pair in stacks[0].pairs for c in pair]
    narrow = [load_narrow(0)]
    pieces = {}
    for c in order:
        at = pl.ds(c * step, step)
        pieces[c] = load(sources[0][0].at[at], weights.at[0, at])
    norm_loads = [load(norm_train, norms.at[0]), load(norm_step, norms.at[1])]
    wide = {}
    for i in (1, 2):
        narrow.append(load_narrow(i))
        wide[i] = load(sources[i][0], weights.at[i])

    turned = [None] * 3

    def merge(i, first, count, put):
        if turned[i] is None:
            for dma in narrow[i]:
                dma.wait()
            turned[i] = lefts[i].T
            if i:
                wide[i].wait()
        lhs = turned[i][first:first + count]
        for t in range(0, columns, TILE):
            cols = pl.ds(t, min(TILE, columns - t))
            product = jnp.dot(lhs, rights[i, :, cols], preferred_element_type=jnp.float32)
            put(cols, merged(weights[i, pl.ds(first, count), cols], product))

    def merge_down(c):
        pieces[c].wait()
        at = pl.ds(pl.multiple_of(me * rows + c * step, 16), step)

        def put(cols, value):
            held[at, cols] = value

        merge(0, c * step, step, put)

    def merge_stage(s, first, count):
        low = sum(spans[:s]) + first
        while count:
            i, at = 1 + low // rows, low % rows
            size = min(count, rows - at)

            def put(cols, value, first=first, size=size):
                if s:
                    owns[s - 1][pl.ds(first, size), cols] = value
                else:
                    block[me, pl.ds(first, size), cols] = value

            merge(i, at, size, put)
            low, first, count = low + size, first + size, count - size

    c, d = stacks[0].pairs[0]
    merge_down(c)
    merge_down(d)
    pl.semaphore_wait(barrier, len(peers))

    def pass_gains(k, first, count):
        part = gains.at[pl.ds(first, count)]
        dma = pltpu.make_async_remote_copy(
            src_ref=part, dst_ref=part, send_sem=n_send.at[k], recv_sem=n_recv.at[k],
            device_id=peers[k], device_id_type=MESH,
        )
        dma.start()
        return dma

    sent = []

    def go(dma):
        dma.start()
        sent.append(dma)

    go(stacks[0].on_x(c))
    go(stacks[0].on_y(d))
    place = mine * GROUP + me
    for dma in norm_loads:
        dma.wait()
    size = norm_train.shape[1]
    gains[place, :, 0:size] = norms[0] + norms[1]
    passed = [pass_gains(k, place, 1) for k in range(len(z.group))]
    for i, stack in enumerate(stacks):
        for k, (c, d) in enumerate(stack.pairs):
            if i:
                merge_stage(0, c * step_1, step_1)
                go(stack.on_x(c))
                merge_stage(0, d * step_1, step_1)
                go(stack.on_y(d))
            elif k:
                merge_down(c)
                go(stack.on_x(c))
                merge_down(d)
                go(stack.on_y(d))
        for c, d in stack.pairs:
            go(stack.on_x(d))
            go(stack.on_y(c))
        for c in range(stack.count):
            go(stack.share(0, me, c))
    for s in range(1, len(STAGES)):
        size = spans[s] // COUNTS[s]
        for c in range(COUNTS[s]):
            merge_stage(s, c * size, size)

    for dma in passed:
        dma.wait_recv()
    for k in range(len(z.group), len(peers)):
        width = 1 << (k - len(z.group))
        passed.append(pass_gains(k, lax.div(mine, width) * (width * GROUP), width * GROUP))
        passed[-1].wait_recv()
    sent += passed

    def turn(owner):
        base = pl.multiple_of(lax.div(owner, 2) * (2 * rows), LANES)

        @pl.loop(0, columns // LANES)
        def _(t):
            cols = pl.ds(pl.multiple_of(t * LANES, LANES), LANES)
            down[cols, pl.ds(base, 2 * rows)] = held[pl.ds(base, 2 * rows), cols].T

    for i, stack in enumerate(stacks):
        for c, d in stack.pairs:
            start = go if i == 0 else lambda dma: dma.start()
            stack.on_x(c).wait_recv()
            start(stack.forward_y(c))
            go(stack.share(1, z.across_x, c))
            stack.on_y(d).wait_recv()
            start(stack.forward_x(d))
            go(stack.share(2, z.across_y, d))
        for c, d in stack.pairs:
            stack.on_x(d).wait_recv()
            go(stack.share(1, z.across_x, d))
            stack.on_y(c).wait_recv()
            go(stack.share(2, z.across_y, c))
        for slot, owner in ((0, me), (1, z.across_x), (2, z.across_y)):
            stack.shared(slot, z.other_core(owner))
            if i == 0:
                turn(owner)
    for i, stack in enumerate(stacks):
        for c, d in stack.pairs:
            if i == 1 and (c, d) == stack.pairs[-1]:
                for e, f in stack.pairs:
                    stack.forward_y(e).wait_send()
                    stack.forward_x(f).wait_send()

                @pl.when(z.core == 1)
                def _():
                    ahead.start()
            stack.forward_y(c).wait_recv()
            go(stack.share(3, z.across, c))
            stack.forward_x(d).wait_recv()
            go(stack.share(3, z.across, d))
        if i == 0:
            stack.shared(3, z.other_core(z.across))
            turn(z.across)
    stacks[1].shared(3, z.other_core(z.across))
    for dma in sent:
        dma.wait_send()

    @pl.when(z.core == 1)
    def _():
        ahead.finish()


def landing(s):
    return 3 if PASSED[s] else 2


def first(sources, norms, tp):
    rows, columns = sources[0].shape
    spans = stage_rows(rows)
    dma = pltpu.SemaphoreType.DMA
    stages = GROUP - 1 + tp.bit_length() - 1
    return pl.pallas_call(
        functools.partial(first_kernel, tp),
        out_shape=(
            pltpu.VMEM((GROUP, spans[0], columns), jnp.bfloat16),
            pltpu.VMEM((columns, rows * GROUP), jnp.bfloat16),
            *(pltpu.VMEM((span, columns), jnp.bfloat16) for span in spans[1:]),
            pltpu.VMEM((landing(1), spans[1], columns), jnp.bfloat16),
            pltpu.VMEM((GROUP * tp, 1, LANES), jnp.float32),
        ),
        in_specs=[ANY] * 11,
        out_specs=[VMEM] * (len(STAGES) + 3),
        scratch_shapes=[
            pltpu.VMEM((rows * GROUP, columns), jnp.bfloat16),
            pltpu.VMEM((3, rows, columns), jnp.bfloat16),
            pltpu.VMEM((3, *sources[1].shape), jnp.bfloat16),
            pltpu.VMEM((3, *sources[2].shape), jnp.bfloat16),
            pltpu.VMEM((2, *norms[0].shape), jnp.float32),
            dma((CHUNKS + 10,)),
            dma((stages,)), dma((stages,)),
            *Stack.sems(CHUNKS), *Stack.sems(COUNTS[0]), *Ahead.sems(1),
        ],
        compiler_params=pltpu.CompilerParams(
            collective_id=0, has_side_effects=True, vmem_limit_bytes=GRANT
        ),
        name="gather_first",
    )(*sources, *norms)


def later_kernel(s, *refs):
    refs = list(refs)

    def take(count):
        taken, refs[:] = refs[:count], refs[count:]
        return taken

    last = s == len(STAGES) - 1
    own, landed, after = take(3)
    own_next = None if last else take(1)[0]
    block = take(1)[0]
    landed_next = None if last else take(1)[0]
    ready, clear, l_sems = take(3)
    count = COUNTS[s]
    step = own.shape[0] // count
    z = Place()
    me = z.me

    def part(owner, c):
        return block.at[owner, pl.ds(c * step, step)]

    stack = Stack(z, part, count, take(10))
    ahead = None if last else Ahead(z, own_next, landed_next, s + 1, take(8))
    done, rest = stack.pairs[:PASSED[s]], stack.pairs[PASSED[s]:]

    barrier = pltpu.get_barrier_semaphore()
    for peer in (z.across_x, z.across_y):
        pl.semaphore_signal(barrier, inc=1, device_id={"zero": peer}, device_id_type=MESH)

    @pl.when(z.core == 0)
    def _():
        pl.semaphore_signal(
            barrier, inc=1, device_id={"zero": z.partner}, device_id_type=MESH
        )

    pl.semaphore_wait(barrier, 2 + z.core)

    def kept(slot, c):
        at = pl.ds(c * step, step)
        return landed.at[slot - 1, at] if slot else own.at[at]

    owners = (me, z.across_x, z.across_y)

    def move(slot):
        src = landed.at[slot - 1] if slot else own
        return pltpu.make_async_copy(src, block.at[owners[slot]], l_sems.at[slot])

    def move_passed(c):
        at = pl.ds(c * step, step)
        return pltpu.make_async_copy(landed.at[2, at], part(z.across, c), l_sems.at[3 + c])

    def arrive(c, d):
        stack.forward_y(c).wait_recv()
        stack.share(3, z.across, c).start()
        stack.forward_x(d).wait_recv()
        stack.share(3, z.across, d).start()

    def sent(pairs):
        for c, d in pairs:
            stack.forward_y(c).wait_send()
            stack.forward_x(d).wait_send()

    @pl.when(z.core == 0)
    def _():
        for c, d in stack.pairs:
            stack.on_x(c, kept(0, c)).start()
            stack.on_y(d, kept(0, d)).start()
        for c, d in stack.pairs:
            stack.on_x(d, kept(0, d)).start()
            stack.on_y(c, kept(0, c)).start()
        move(0).start()
        for c, d in stack.pairs:
            stack.on_x(c).wait_recv()
            stack.forward_y(c).start()
            stack.on_y(d).wait_recv()
            stack.forward_x(d).start()
        for c, d in stack.pairs:
            stack.on_x(d).wait_recv()
            stack.on_y(c).wait_recv()
        pl.semaphore_wait(ready, 1)
        for c in range(count):
            stack.share(0, me, c, kept(0, c)).start()
        for slot in (1, 2):
            for c in range(count):
                stack.share(slot, owners[slot], c).start()
        for c in range(count):
            stack.on_x(c).wait_send()
            stack.on_y(c).wait_send()
        move(0).wait()
        for c, d in done:
            arrive(c, d)
        sent(done)

    @pl.when(z.core == 1)
    def _():
        pl.semaphore_signal(
            ready, inc=1, device_id={"zero": z.partner}, device_id_type=MESH
        )
        for c, d in rest:
            stack.forward_y(c, kept(1, c)).start()
            stack.forward_x(d, kept(2, d)).start()
        for slot, owner in enumerate(owners):
            for c in range(count):
                stack.share(slot, owner, c, kept(slot, c)).start()
        passed = [c for pair in done for c in pair]
        for c in passed:
            stack.share(3, z.across, c, landed.at[2, pl.ds(c * step, step)]).start()
        moves = [move(slot) for slot in range(3)] + [move_passed(c) for c in passed]
        for dma in moves:
            dma.start()
        for dma in moves:
            dma.wait()

    for c, d in rest[:-1]:
        arrive(c, d)
    sent(rest)
    if ahead is not None:
        @pl.when(z.core == 0)
        def _():
            pl.semaphore_signal(
                clear, inc=1, device_id={"zero": z.partner}, device_id_type=MESH
            )

        @pl.when(z.core == 1)
        def _():
            pl.semaphore_wait(clear, 1)
            ahead.start()
    for c, d in rest[-1:]:
        arrive(c, d)
    for slot, owner in enumerate((*owners, z.across)):
        stack.shared(slot, z.other_core(owner))
        for c in range(count):
            stack.share(slot, owner, c).wait_send()
    if ahead is not None:
        @pl.when(z.core == 1)
        def _():
            ahead.finish()


def in_vmem(*arrays):
    return [pltpu.with_memory_space_constraint(a, pltpu.VMEM) for a in arrays]


def later(s, owns, landed, after):
    last = s == len(STAGES) - 1
    own = owns[s - 1]
    span, columns = own.shape
    outs = [pltpu.VMEM((GROUP, span, columns), jnp.bfloat16)]
    ahead = []
    if not last:
        outs.append(pltpu.VMEM((landing(s + 1), *owns[s].shape), jnp.bfloat16))
        ahead = Ahead.sems(s + 1)
    operands = [*in_vmem(own, landed, after), *([] if last else in_vmem(owns[s]))]
    return pl.pallas_call(
        functools.partial(later_kernel, s),
        out_shape=tuple(outs),
        in_specs=[VMEM] * len(operands),
        out_specs=[VMEM] * len(outs),
        scratch_shapes=[
            pltpu.SemaphoreType.REGULAR, pltpu.SemaphoreType.REGULAR,
            pltpu.SemaphoreType.DMA((3 + COUNTS[s],)),
            *Stack.sems(COUNTS[s]), *ahead,
        ],
        compiler_params=pltpu.CompilerParams(
            collective_id=s, has_side_effects=True, vmem_limit_bytes=2**20
        ),
        name=f"gather_{s}",
    )(*operands)


def lay_norm(tp, size, gains, lines, laid):
    lane = lax.broadcasted_iota(jnp.int32, (1, LANES), 1)
    parts = [[] for _ in range(lines.shape[0])]
    for k in range(GROUP * tp):
        zero, z = divmod(k, tp)
        piece = jnp.where(lane < size, gains[z * GROUP + zero], 0.0)
        line, shift = divmod(k * size, LANES)
        piece = pltpu.roll(piece, shift, 1) if shift else piece
        parts[line].append(jnp.where(lane >= shift, piece, 0.0))
        if shift + size > LANES:
            parts[line + 1].append(jnp.where(lane < shift, piece, 0.0))
    for line, terms in enumerate(parts):
        lines[pl.ds(line, 1), :] = sum(terms[1:], terms[0])
    laid[...] = lines[...].astype(jnp.bfloat16)


def store_kernel(pieces, rows, targets, started, follows, norm_of, *refs):
    refs = list(refs)
    block = refs.pop(0)
    down = gains = None
    if norm_of:
        down, gains = refs.pop(0), refs.pop(0)
    del refs[:started]
    outs = {name: refs.pop(0) for name in targets}
    copies = []

    def go(src, dst):
        copies.append(pltpu.make_async_copy(src, dst, refs[-1].at[len(copies)]))
        copies[-1].start()

    token = refs.pop(0) if follows else None
    if norm_of:
        down_out, norm, lines, laid = (refs.pop(0) for _ in range(4))
        quarter = down.shape[0] // 4
        for k in range(4):
            at = pl.ds(k * quarter, quarter)
            go(down.at[at], down_out.at[at])
    for owner in range(GROUP):
        for name, src, dst, count in pieces:
            go(
                block.at[owner, pl.ds(src, count)],
                outs[name].at[pl.ds(owner * rows + dst, count)],
            )
    if norm_of:
        lay_norm(*norm_of, gains, lines, laid)
        go(laid, norm)
    if follows:
        token[...] = jnp.zeros_like(token)
    for copy in copies:
        copy.wait()


def store(s, block, rows, made, down=None, gains=None, tp=None, size=None):
    columns = block.shape[2]
    spans = stage_rows(rows)
    low, high = sum(spans[:s]), sum(spans[:s + 1])
    pieces = []
    for k, name in enumerate(("gate", "up")):
        a, b = max(low, k * rows), min(high, (k + 1) * rows)
        if a < b:
            pieces.append((name, a - low, a - k * rows, b - a))
    targets = [name for name, *_ in pieces]
    names = [*targets, "token"] if s < len(STAGES) - 1 else targets
    whole = jax.ShapeDtypeStruct((rows * GROUP, columns), jnp.bfloat16)
    last = s == len(STAGES) - 1
    outs = [whole] * len(targets) + [pltpu.VMEM((8, LANES), jnp.float32)] * (not last)
    operands = in_vmem(block) if down is None else in_vmem(block, down, gains)
    in_specs = [VMEM] * len(operands)
    out_specs = [ANY] * len(targets) + [VMEM] * (not last)
    aliases = {}
    for k, name in enumerate(targets):
        if name in made:
            aliases[len(operands)] = k
            operands.append(made[name])
            in_specs.append(ANY)
    copies = GROUP * len(pieces)
    scratch = []
    if down is not None:
        lines = (GROUP * tp * size // LANES, LANES)
        outs += [jax.ShapeDtypeStruct(down.shape, down.dtype),
                 jax.ShapeDtypeStruct(lines, jnp.bfloat16)]
        out_specs += [ANY, ANY]
        scratch += [pltpu.VMEM(lines, jnp.float32), pltpu.VMEM(lines, jnp.bfloat16)]
        copies += 5
        names += ["down", "norm"]
    results = pl.pallas_call(
        functools.partial(
            store_kernel, pieces, rows, targets, len(aliases), not last,
            (tp, size) if tp else None,
        ),
        out_shape=tuple(outs),
        in_specs=in_specs,
        out_specs=out_specs,
        scratch_shapes=[*scratch, pltpu.SemaphoreType.DMA((copies,))],
        input_output_aliases=aliases,
        compiler_params=pltpu.CompilerParams(vmem_limit_bytes=2**20),
        name=f"store_{s}",
    )(*operands)
    return {**made, **dict(zip(names, results))}


def local(
    weight_gate, low_gate, high_gate,
    weight_up, low_up, high_up,
    weight_down, low_down, high_down,
    norm_train, norm_step,
    *, fast, tp,
):
    sources = (
        (weight_down.T, high_down, low_down.T),
        (weight_gate, low_gate.T, high_gate),
        (weight_up, low_up.T, high_up),
    )
    if fast:
        rows = weight_gate.shape[0]
        norms = (norm_train[None], norm_step[None])
        block, down, *owns, landed, gains = first(sum(sources, ()), norms, tp)
        made = store(0, block, rows, {}, down, gains, tp, norm_train.shape[0])
        for s in range(1, len(STAGES)):
            block, *rest = later(s, owns, landed, made["token"])
            made = store(s, block, rows, made)
            landed = rest[0] if rest else None
        ready_gate, ready_up, ready_down = made["gate"], made["up"], made["down"]
        serve_norm = made["norm"].reshape(-1)
    else:
        down, gate, up = (merge_rows(*s) for s in sources)
        ready_gate, ready_up, ready_down = (
            lax.all_gather(a, "zero", axis=0, tiled=True) for a in (gate, up, down)
        )
        ready_down = ready_down.T
        serve_norm = lax.all_gather(
            (norm_train + norm_step).astype(jnp.bfloat16), ("zero", "tp"), axis=0, tiled=True
        )
    return (ready_gate, ready_up, ready_down, serve_norm)


def solution(mesh):
    def step(*args):
        zero, tp = mesh.shape["zero"], mesh.shape["tp"]
        rows, columns = args[0].shape[0] // zero, args[0].shape[1] // tp
        fast = (
            zero == GROUP
            and tp & (tp - 1) == 0
            and args[9].shape[0] <= zero * tp * LANES
            and args[9].shape[0] % LANES == 0
            and rows % (16 * CHUNKS) == 0
            and all(
                2 * rows * share % (8 * count * sum(STAGES)) == 0
                for share, count in zip(STAGES, COUNTS)
            )
            and columns % LANES == 0
            and 2 * rows % LANES == 0
            and args[6].shape == args[0].shape[::-1]
        )
        return jax.shard_map(
            functools.partial(local, fast=fast, tp=tp),
            mesh=mesh,
            in_specs=(
                P("zero", "tp"), P("zero", None), P(None, "tp"),
                P("zero", "tp"), P("zero", None), P(None, "tp"),
                P("tp", "zero"), P("tp", None), P(None, "zero"),
                P(("zero", "tp")), P(("zero", "tp")),
            ),
            out_specs=(P(None, "tp"), P(None, "tp"), P("tp", None), P()),
            check_vma=False,
        )(*args)

    return step
```

time: 165 us -> 162 us (0.982)
  Pallas kernels: 164 us -> 161 us
    pallas_call x1, Pallas kernels: 111 us -> 100 us  [first(): pl.pallas_call(functools.partial(first_kernel, tp), out_shape=(pltpu.VMEM...]
    pallas_call x3 -> x5, Pallas kernels: 53.1 us -> 61.4 us  [the longest x2 47.4 us: later(): pl.pallas_call(functools.partial(later_kernel, s), out_shape=tuple(outs),...]
where the time goes in v2:
time: 162 us
  Pallas kernels  161 us (99%)
    pallas_call x1, Pallas kernels, first(): pl.pallas_call(functools.partial(first_kernel, tp), out_shape=(pltpu.VMEM...  100 us
    pallas_call x2, Pallas kernels, later(): pl.pallas_call(functools.partial(later_kernel, s), out_shape=tuple(outs),...  47.4 us
    pallas_call x3, Pallas kernels, store(): pl.pallas_call(functools.partial(store_kernel, pieces, rows, targets, len...  14 us

profile of v2, /device:TPU:0, one launch (start us, length us, event | category | flops | bytes accessed | tf_op | source)
XLA Modules:
  0.0 162.0 jit_solution(16188770164834385778)
XLA Ops:
  0.6 100.0 %gather_first.1 = (bf16[8,256,2432]{2,1,0:T(8,128)(2,1)S(1)}, bf16[2432,2560]{1,0:T(8,128)(2,1)S(1)}, bf16[256,2432]{1,0:T(8,128)(2,1)S(1)}, bf16[128,2432]{1,0:...) custom-call(bf16[320,2432]{1,0:T(8,128)(2,1)} %bitcast.7, bf16[16,320]{1,0:T(8,128)(2,1)} %refs_1_.1, ...), custom_call_target="tpu_custom_call" | custom-call | tf_op jit(solution)/shard_map/gather_first/pallas_call | solution.py:410
  100.6 7.7 %store_0.1 = (bf16[2560,2432]{1,0:T(8,128)(2,1)}, f32[8,128]{1,0:T(8,128)S(1)}, bf16[2432,2560]{1,0:T(8,128)(2,1)}, bf16[20,128]{1,0:T(8,128)(2,1)}) custom-call(bf16[8,256,2432]{2,1,0:T(8,128)(2,1)S(1)} %get-tuple-element.21.refs_0_, bf16[2432,2560]{1,0:T(8,128)(2,1)S(1)} %get-tuple-element.22.refs_1_, f32[32,1,128]{2,1,0:T(1,128)S(1)} %get-tuple-element.23.refs_2_), custom_call_target="tpu_custom_call" | custom-call | tf_op jit(solution)/shard_map/store_0/pallas_call | solution.py:693
  108.3 31.0 %gather_1.1 = (bf16[8,256,2432]{2,1,0:T(8,128)(2,1)S(1)}, bf16[3,128,2432]{2,1,0:T(8,128)(2,1)S(1)}) custom-call(bf16[256,2432]{1,0:T(8,128)(2,1)S(1)} %get-tuple-element.19.refs_0_, bf16[3,256,2432]{2,1,0:T(8,128)(2,1)S(1)} %get-tuple-element.20.refs_1_, f32[8,128]{1,0:T(8,128)S(1)} %get-tuple-element.24.refs_2_, ...), custom_call_target="tpu_custom_call" | custom-call | tf_op jit(solution)/shard_map/gather_1/pallas_call | solution.py:591
  139.3 3.9 %store_1.1 = (bf16[2560,2432]{1,0:T(8,128)(2,1)}, bf16[2560,2432]{1,0:T(8,128)(2,1)}, f32[8,128]{1,0:T(8,128)S(1)}) custom-call(bf16[8,256,2432]{2,1,0:T(8,128)(2,1)S(1)} %get-tuple-element.26.refs_0_, bf16[2560,2432]{1,0:T(8,128)(2,1)} %get-tuple-element.27.refs_1_), custom_call_target="tpu_custom_call", output_to_operand_aliasing={{0}: (1, {})} | custom-call | tf_op jit(solution)/shard_map/store_1/pallas_call | solution.py:693
  143.3 16.4 %gather_2.1.refs_0_ = bf16[8,128,2432]{2,1,0:T(8,128)(2,1)S(1)} custom-call(bf16[128,2432]{1,0:T(8,128)(2,1)S(1)} %get-tuple-element.25.refs_3_.refs_0_, bf16[3,128,2432]{2,1,0:T(8,128)(2,1)S(1)} %get-tuple-element.29.refs_1_, f32[8,128]{1,0:T(8,128)S(1)} %get-tuple-element.30.refs_2_), custom_call_target="tpu_custom_call" | custom-call | tf_op jit(solution)/shard_map/gather_2/pallas_call | solution.py:591
  159.7 2.3 %store_2.1 = bf16[2560,2432]{1,0:T(8,128)(2,1)} custom-call(bf16[8,128,2432]{2,1,0:T(8,128)(2,1)S(1)} %gather_2.1.refs_0_, bf16[2560,2432]{1,0:T(8,128)(2,1)} %get-tuple-element.31.refs_1_), custom_call_target="tpu_custom_call", output_to_operand_aliasing={{}: (1, {})} | custom-call | tf_op jit(solution)/shard_map/store_2/pallas_call | solution.py:693

commit v3 on v2

--- a/solution.py
+++ b/solution.py
@@ -72,115 +72,132 @@
 
 
 class Stack:
-    def __init__(self, z, part, count, sems):
-        self.z, self.part, self.count, self.half = z, part, count, count // 2
-        (self.x_send, self.x_recv, self.y_send, self.y_recv,
-         self.fx_send, self.fx_recv, self.fy_send, self.fy_recv,
-         self.p_send, self.p_recv) = sems
+    def __init__(self, z, part, whole, count, sems):
+        self.z, self.part, self.whole = z, part, whole
+        self.count, self.half = count, count // 2
+        self.sent, self.x, self.y, self.f_x, self.f_y, self.p = sems
         self.pairs = list(zip(range(self.half), range(self.half, count)))
 
     @staticmethod
     def sems(count):
-        dma = pltpu.SemaphoreType.DMA
-        return [dma((count,))] * 4 + [dma((count // 2,))] * 4 + [dma((4, count))] * 2
-
-    def copy(self, owner, c, peer, send, recv, src=None):
-        ref = self.part(owner, c)
-        return remote(ref if src is None else src, ref, peer, send, recv)
+        dma, half = pltpu.SemaphoreType.DMA, count // 2
+        return [
+            dma((3,)), dma((half + 1,)), dma((half + 1,)), dma((half,)), dma((half,)), dma((4,))
+        ]
+
+    def copy(self, owner, c, n, peer, sent, recv, src=None):
+        ref = self.part(owner, c, n)
+        return remote(ref if src is None else src, ref, peer, self.sent.at[sent], recv)
 
     def on_x(self, c, src=None):
+        return self.copy(
+            self.z.me, c, 1, self.z.across_x, 0, self.x.at[min(c, self.half)], src
+        )
+
+    def on_y(self, c, src=None):
+        at = c - self.half if c >= self.half else self.half
+        return self.copy(self.z.me, c, 1, self.z.across_y, 0, self.y.at[at], src)
+
+    def wait_late_x(self):
+        half = self.half
+        self.copy(self.z.across_x, half, half, self.z.across_x, 0, self.x.at[half]).wait_recv()
+
+    def wait_early_y(self):
+        half = self.half
+        self.copy(self.z.across_y, 0, half, self.z.across_y, 0, self.y.at[half]).wait_recv()
+
+    def forward_x(self, d, src=None):
         z = self.z
-        return self.copy(z.me, c, z.across_x, self.x_send.at[c], self.x_recv.at[c], src)
-
-    def on_y(self, c, src=None):
-        z = self.z
-        return self.copy(z.me, c, z.across_y, self.y_send.at[c], self.y_recv.at[c], src)
-
-    def forward_x(self, c, src=None):
-        z, k = self.z, c - self.half
-        return self.copy(z.across_y, c, z.across_x, self.fx_send.at[k], self.fx_recv.at[k], src)
+        return self.copy(z.across_y, d, 1, z.across_x, 1, self.f_x.at[d - self.half], src)
 
     def forward_y(self, c, src=None):
         z = self.z
-        return self.copy(z.across_x, c, z.across_y, self.fy_send.at[c], self.fy_recv.at[c], src)
-
-    def share(self, slot, owner, c, src=None):
-        return self.copy(
-            owner, c, self.z.partner, self.p_send.at[slot, c], self.p_recv.at[slot, c], src
-        )
+        return self.copy(z.across_x, c, 1, z.across_y, 1, self.f_y.at[c], src)
+
+    def share(self, slot, owner, c, n, src=None):
+        return self.copy(owner, c, n, self.z.partner, 2, self.p.at[slot], src)
 
     def shared(self, slot, owner):
-        for c in range(self.count):
-            self.share(slot, owner, c).wait_recv()
+        self.share(slot, owner, 0, self.count).wait_recv()
+
+    def wait_sent(self, kind, ref):
+        remote(ref, ref, self.z.partner, self.sent.at[kind], self.p.at[0]).wait_send()
+
+    def wait_own(self):
+        self.wait_sent(0, self.whole(2))
+
+    def wait_forwards(self, passed=0):
+        if 2 * passed < self.count:
+            self.wait_sent(1, self.part(self.z.me, 0, self.count - 2 * passed))
+
+    def wait_shares(self):
+        self.wait_sent(2, self.whole(4))
 
 
 class Ahead:
     def __init__(self, z, own, landed, s, sems):
         self.z, self.own, self.landed = z, own, landed
         self.count, self.step = COUNTS[s], own.shape[0] // COUNTS[s]
-        (self.x_send, self.x_recv, self.y_send, self.y_recv,
-         self.fx_send, self.fx_recv, self.fy_send, self.fy_recv) = sems
-        self.pairs = list(zip(range(self.count // 2), range(self.count // 2, self.count)))
-        self.passed = list(enumerate(self.pairs[:PASSED[s]]))
+        self.half, self.passed = self.count // 2, PASSED[s]
+        self.sent, self.x, self.y, self.f = sems
 
     @staticmethod
     def sems(s):
         dma = pltpu.SemaphoreType.DMA
-        return [dma((COUNTS[s],))] * 4 + [dma((max(PASSED[s], 1),))] * 4
-
-    def at(self, c):
-        return pl.ds(c * self.step, self.step)
+        return [dma((2,)), dma((PASSED[s] + 1,)), dma((PASSED[s] + 1,)), dma((1,))]
+
+    def at(self, c, n=1):
+        return pl.ds(c * self.step, n * self.step)
 
     def on_x(self, c):
         return remote(
             self.own.at[self.at(c)], self.landed.at[0, self.at(c)], self.z.across_x,
-            self.x_send.at[c], self.x_recv.at[c],
+            self.sent.at[0], self.x.at[min(c, self.passed)],
         )
 
     def on_y(self, c):
+        k = c - self.half
         return remote(
             self.own.at[self.at(c)], self.landed.at[1, self.at(c)], self.z.across_y,
-            self.y_send.at[c], self.y_recv.at[c],
-        )
-
-    def pass_y(self, k, c):
+            self.sent.at[0], self.y.at[k if 0 <= k < self.passed else self.passed],
+        )
+
+    def pass_y(self, c):
         return remote(
             self.landed.at[0, self.at(c)], self.landed.at[2, self.at(c)], self.z.across_y,
-            self.fy_send.at[k], self.fy_recv.at[k],
-        )
-
-    def pass_x(self, k, d):
+            self.sent.at[1], self.f.at[0],
+        )
+
+    def pass_x(self, d):
         return remote(
             self.landed.at[1, self.at(d)], self.landed.at[2, self.at(d)], self.z.across_x,
-            self.fx_send.at[k], self.fx_recv.at[k],
+            self.sent.at[1], self.f.at[0],
         )
 
     def start(self):
-        for c, d in self.pairs:
+        half = self.half
+        for c in range(half):
             self.on_x(c).start()
-            self.on_y(d).start()
-        for c, d in self.pairs:
-            self.on_x(d).start()
+            self.on_y(half + c).start()
+        for c in range(half):
+            self.on_x(half + c).start()
             self.on_y(c).start()
 
     def finish(self):
-        for k, (c, d) in self.passed:
+        z, passed = self.z, self.passed
+        for c in range(passed):
             self.on_x(c).wait_recv()
-            self.pass_y(k, c).start()
-            self.on_y(d).wait_recv()
-            self.pass_x(k, d).start()
-        early = [c for _, (c, _) in self.passed]
-        late = [d for _, (_, d) in self.passed]
-        for c in range(self.count):
-            self.on_x(c).wait_send()
-            self.on_y(c).wait_send()
-            if c not in early:
-                self.on_x(c).wait_recv()
-            if c not in late:
-                self.on_y(c).wait_recv()
-        for k, (c, d) in self.passed:
-            self.pass_y(k, c).wait()
-            self.pass_x(k, d).wait()
+            self.pass_y(c).start()
+            self.on_y(self.half + c).wait_recv()
+            self.pass_x(self.half + c).start()
+        both = self.landed.at[pl.ds(0, 2)]
+        remote(both, both, z.across_x, self.sent.at[0], self.f.at[0]).wait_send()
+        rest = self.landed.at[0, self.at(0, self.count - passed)]
+        for sem in (self.x, self.y):
+            remote(rest, rest, z.across_x, self.sent.at[0], sem.at[passed]).wait_recv()
+        if passed:
+            some = self.landed.at[2, self.at(0, 2 * passed)]
+            remote(some, some, z.across_x, self.sent.at[1], self.f.at[0]).wait()
 
 
 def first_kernel(tp, *refs):
@@ -196,7 +213,7 @@
     block, down = take(2)
     owns = take(kept)
     landed, gains = take(2)
-    held, weights, lefts, rights, norms, w_sems, n_send, n_recv = take(8)
+    held, weights, lefts, rights, norms, w_sems, n_sent, n_recv, met = take(9)
     rows, columns = sources[1][0].shape
     step = rows // CHUNKS
     z = Place()
@@ -204,27 +221,39 @@
     spans = stage_rows(rows)
     step_1 = spans[0] // COUNTS[0]
 
-    def held_part(owner, c):
-        return held.at[pl.ds(pl.multiple_of(owner * rows + c * step, 16), step), :]
-
-    def block_part(owner, c):
-        return block.at[owner, pl.ds(c * step_1, step_1)]
+    def held_part(owner, c, n):
+        return held.at[pl.ds(pl.multiple_of(owner * rows + c * step, 16), n * step), :]
+
+    def held_whole(n):
+        return held.at[pl.ds(0, n * rows), :]
+
+    def block_part(owner, c, n):
+        return block.at[owner, pl.ds(c * step_1, n * step_1)]
+
+    def block_whole(n):
+        return block.at[pl.ds(0, n)]
 
     stacks = (
-        Stack(z, held_part, CHUNKS, take(10)), Stack(z, block_part, COUNTS[0], take(10))
+        Stack(z, held_part, held_whole, CHUNKS, take(6)),
+        Stack(z, block_part, block_whole, COUNTS[0], take(6)),
     )
-    ahead = Ahead(z, owns[0], landed, 1, take(8))
+    ahead = Ahead(z, owns[0], landed, 1, take(4))
 
     mine = lax.axis_index("tp")
-    peers, width = [{"zero": peer} for peer in z.group], 1
+    near = [{"zero": peer} for peer in z.group]
+    far, width = [], 1
     while width < tp:
         bit = lax.rem(lax.div(mine, width), 2)
-        peers.append({"tp": mine + width - 2 * width * bit})
+        far.append((bit, {"tp": mine + width - 2 * width * bit}))
         width *= 2
 
     barrier = pltpu.get_barrier_semaphore()
-    for peer in peers:
+    for peer in near:
         pl.semaphore_signal(barrier, inc=1, device_id=peer, device_id_type=MESH)
+    for bit, peer in far:
+        @pl.when(bit == 0)
+        def _():
+            pl.semaphore_signal(barrier, inc=1, device_id=peer, device_id_type=MESH)
 
     loads = []
 
@@ -243,7 +272,12 @@
     for c in order:
         at = pl.ds(c * step, step)
         pieces[c] = load(sources[0][0].at[at], weights.at[0, at])
-    norm_loads = [load(norm_train, norms.at[0]), load(norm_step, norms.at[1])]
+    norm_loads = [
+        pltpu.make_async_copy(src, norms.at[k], w_sems.at[CHUNKS + 8])
+        for k, src in enumerate((norm_train, norm_step))
+    ]
+    for dma in norm_loads:
+        dma.start()
     wide = {}
     for i in (1, 2):
         narrow.append(load_narrow(i))
@@ -290,61 +324,63 @@
 
     c, d = stacks[0].pairs[0]
     merge_down(c)
+    pl.semaphore_wait(barrier, len(near) + sum(bit for bit, _ in far))
+    stacks[0].on_x(c).start()
     merge_down(d)
-    pl.semaphore_wait(barrier, len(peers))
-
-    def pass_gains(k, first, count):
-        part = gains.at[pl.ds(first, count)]
-        dma = pltpu.make_async_remote_copy(
-            src_ref=part, dst_ref=part, send_sem=n_send.at[k], recv_sem=n_recv.at[k],
-            device_id=peers[k], device_id_type=MESH,
-        )
-        dma.start()
-        return dma
-
-    sent = []
-
-    def go(dma):
-        dma.start()
-        sent.append(dma)
-
-    go(stacks[0].on_x(c))
-    go(stacks[0].on_y(d))
+    stacks[0].on_y(d).start()
+
     place = mine * GROUP + me
-    for dma in norm_loads:
-        dma.wait()
+    pltpu.make_async_copy(norms, norms, w_sems.at[CHUNKS + 8]).wait()
     size = norm_train.shape[1]
     gains[place, :, 0:size] = norms[0] + norms[1]
-    passed = [pass_gains(k, place, 1) for k in range(len(z.group))]
+
+    def pass_gains(k, peer, first, count):
+        part = gains.at[pl.ds(first, count)]
+        return pltpu.make_async_remote_copy(
+            src_ref=part, dst_ref=part, send_sem=n_sent.at[0], recv_sem=n_recv.at[k],
+            device_id=peer, device_id_type=MESH,
+        )
+
+    for k, peer in enumerate(near):
+        pass_gains(k, peer, place, 1).start()
+    for k, (bit, peer) in enumerate(far):
+        @pl.when(bit == 1)
+        def _():
+            pl.semaphore_signal(met.at[k], inc=1, device_id=peer, device_id_type=MESH)
+
     for i, stack in enumerate(stacks):
         for k, (c, d) in enumerate(stack.pairs):
             if i:
                 merge_stage(0, c * step_1, step_1)
-                go(stack.on_x(c))
+                stack.on_x(c).start()
                 merge_stage(0, d * step_1, step_1)
-                go(stack.on_y(d))
+                stack.on_y(d).start()
             elif k:
                 merge_down(c)
-                go(stack.on_x(c))
+                stack.on_x(c).start()
                 merge_down(d)
-                go(stack.on_y(d))
+                stack.on_y(d).start()
         for c, d in stack.pairs:
-            go(stack.on_x(d))
-            go(stack.on_y(c))
-        for c in range(stack.count):
-            go(stack.share(0, me, c))
+            stack.on_x(d).start()
+            stack.on_y(c).start()
+        stack.share(0, me, 0, stack.count).start()
     for s in range(1, len(STAGES)):
         size = spans[s] // COUNTS[s]
         for c in range(COUNTS[s]):
             merge_stage(s, c * size, size)
 
-    for dma in passed:
+    for k in range(len(near)):
+        pass_gains(k, near[k], place, 1).wait_recv()
+    for k, (bit, peer) in enumerate(far):
+        @pl.when(bit == 0)
+        def _():
+            pl.semaphore_wait(met.at[k], 1)
+        width = 1 << k
+        dma = pass_gains(
+            len(near) + k, peer, lax.div(mine, width) * (width * GROUP), width * GROUP
+        )
+        dma.start()
         dma.wait_recv()
-    for k in range(len(z.group), len(peers)):
-        width = 1 << (k - len(z.group))
-        passed.append(pass_gains(k, lax.div(mine, width) * (width * GROUP), width * GROUP))
-        passed[-1].wait_recv()
-    sent += passed
 
     def turn(owner):
         base = pl.multiple_of(lax.div(owner, 2) * (2 * rows), LANES)
@@ -355,19 +391,18 @@
             down[cols, pl.ds(base, 2 * rows)] = held[pl.ds(base, 2 * rows), cols].T
 
     for i, stack in enumerate(stacks):
+        half = stack.half
         for c, d in stack.pairs:
-            start = go if i == 0 else lambda dma: dma.start()
             stack.on_x(c).wait_recv()
-            start(stack.forward_y(c))
-            go(stack.share(1, z.across_x, c))
+            stack.forward_y(c).start()
+            stack.share(1, z.across_x, c, 1).start()
             stack.on_y(d).wait_recv()
-            start(stack.forward_x(d))
-            go(stack.share(2, z.across_y, d))
-        for c, d in stack.pairs:
-            stack.on_x(d).wait_recv()
-            go(stack.share(1, z.across_x, d))
-            stack.on_y(c).wait_recv()
-            go(stack.share(2, z.across_y, c))
+            stack.forward_x(d).start()
+            stack.share(2, z.across_y, d, 1).start()
+        stack.wait_late_x()
+        stack.share(1, z.across_x, half, half).start()
+        stack.wait_early_y()
+        stack.share(2, z.across_y, 0, half).start()
         for slot, owner in ((0, me), (1, z.across_x), (2, z.across_y)):
             stack.shared(slot, z.other_core(owner))
             if i == 0:
@@ -375,23 +410,29 @@
     for i, stack in enumerate(stacks):
         for c, d in stack.pairs:
             if i == 1 and (c, d) == stack.pairs[-1]:
-                for e, f in stack.pairs:
-                    stack.forward_y(e).wait_send()
-                    stack.forward_x(f).wait_send()
+                stack.wait_forwards()
 
                 @pl.when(z.core == 1)
                 def _():
                     ahead.start()
             stack.forward_y(c).wait_recv()
-            go(stack.share(3, z.across, c))
+            stack.share(3, z.across, c, 1).start()
             stack.forward_x(d).wait_recv()
-            go(stack.share(3, z.across, d))
+            stack.share(3, z.across, d, 1).start()
         if i == 0:
             stack.shared(3, z.other_core(z.across))
             turn(z.across)
+            stack.wait_forwards()
+            stack.wait_own()
+            stack.wait_shares()
+            done = gains.at[pl.ds(0, GROUP * tp - 1)]
+            pltpu.make_async_remote_copy(
+                src_ref=done, dst_ref=done, send_sem=n_sent.at[0], recv_sem=n_recv.at[0],
+                device_id=near[0], device_id_type=MESH,
+            ).wait_send()
     stacks[1].shared(3, z.other_core(z.across))
-    for dma in sent:
-        dma.wait_send()
+    stacks[1].wait_own()
+    stacks[1].wait_shares()
 
     @pl.when(z.core == 1)
     def _():
@@ -406,7 +447,7 @@
     rows, columns = sources[0].shape
     spans = stage_rows(rows)
     dma = pltpu.SemaphoreType.DMA
-    stages = GROUP - 1 + tp.bit_length() - 1
+    far = tp.bit_length() - 1
     return pl.pallas_call(
         functools.partial(first_kernel, tp),
         out_shape=(
@@ -424,8 +465,8 @@
             pltpu.VMEM((3, *sources[1].shape), jnp.bfloat16),
             pltpu.VMEM((3, *sources[2].shape), jnp.bfloat16),
             pltpu.VMEM((2, *norms[0].shape), jnp.float32),
-            dma((CHUNKS + 10,)),
-            dma((stages,)), dma((stages,)),
+            dma((CHUNKS + 9,)), dma((1,)), dma((GROUP - 1 + far,)),
+            pltpu.SemaphoreType.REGULAR((max(far, 1),)),
             *Stack.sems(CHUNKS), *Stack.sems(COUNTS[0]), *Ahead.sems(1),
         ],
         compiler_params=pltpu.CompilerParams(
@@ -453,12 +494,16 @@
     z = Place()
     me = z.me
 
-    def part(owner, c):
-        return block.at[owner, pl.ds(c * step, step)]
-
-    stack = Stack(z, part, count, take(10))
-    ahead = None if last else Ahead(z, own_next, landed_next, s + 1, take(8))
-    done, rest = stack.pairs[:PASSED[s]], stack.pairs[PASSED[s]:]
+    def part(owner, c, n):
+        return block.at[owner, pl.ds(c * step, n * step)]
+
+    def whole(n):
+        return block.at[pl.ds(0, n)]
+
+    stack = Stack(z, part, whole, count, take(6))
+    ahead = None if last else Ahead(z, own_next, landed_next, s + 1, take(4))
+    passed = PASSED[s]
+    rest = stack.pairs[passed:]
 
     barrier = pltpu.get_barrier_semaphore()
     for peer in (z.across_x, z.across_y):
@@ -472,61 +517,45 @@
 
     pl.semaphore_wait(barrier, 2 + z.core)
 
-    def kept(slot, c):
-        at = pl.ds(c * step, step)
+    def kept(slot, c, n):
+        at = pl.ds(c * step, n * step)
         return landed.at[slot - 1, at] if slot else own.at[at]
 
     owners = (me, z.across_x, z.across_y)
 
     def move(slot):
-        src = landed.at[slot - 1] if slot else own
-        return pltpu.make_async_copy(src, block.at[owners[slot]], l_sems.at[slot])
-
-    def move_passed(c):
-        at = pl.ds(c * step, step)
-        return pltpu.make_async_copy(landed.at[2, at], part(z.across, c), l_sems.at[3 + c])
+        return pltpu.make_async_copy(kept(slot, 0, count), block.at[owners[slot]], l_sems.at[0])
 
     def arrive(c, d):
         stack.forward_y(c).wait_recv()
-        stack.share(3, z.across, c).start()
+        stack.share(3, z.across, c, 1).start()
         stack.forward_x(d).wait_recv()
-        stack.share(3, z.across, d).start()
-
-    def sent(pairs):
-        for c, d in pairs:
-            stack.forward_y(c).wait_send()
-            stack.forward_x(d).wait_send()
+        stack.share(3, z.across, d, 1).start()
 
     @pl.when(z.core == 0)
     def _():
         for c, d in stack.pairs:
-            stack.on_x(c, kept(0, c)).start()
-            stack.on_y(d, kept(0, d)).start()
+            stack.on_x(c, kept(0, c, 1)).start()
+            stack.on_y(d, kept(0, d, 1)).start()
         for c, d in stack.pairs:
-            stack.on_x(d, kept(0, d)).start()
-            stack.on_y(c, kept(0, c)).start()
+            stack.on_x(d, kept(0, d, 1)).start()
+            stack.on_y(c, kept(0, c, 1)).start()
         move(0).start()
         for c, d in stack.pairs:
             stack.on_x(c).wait_recv()
             stack.forward_y(c).start()
             stack.on_y(d).wait_recv()
             stack.forward_x(d).start()
-        for c, d in stack.pairs:
-            stack.on_x(d).wait_recv()
-            stack.on_y(c).wait_recv()
+        stack.wait_late_x()
+        stack.wait_early_y()
         pl.semaphore_wait(ready, 1)
-        for c in range(count):
-            stack.share(0, me, c, kept(0, c)).start()
+        stack.share(0, me, 0, count, kept(0, 0, count)).start()
         for slot in (1, 2):
-            for c in range(count):
-                stack.share(slot, owners[slot], c).start()
-        for c in range(count):
-            stack.on_x(c).wait_send()
-            stack.on_y(c).wait_send()
+            stack.share(slot, owners[slot], 0, count).start()
+        stack.wait_own()
         move(0).wait()
-        for c, d in done:
+        for c, d in stack.pairs[:passed]:
             arrive(c, d)
-        sent(done)
 
     @pl.when(z.core == 1)
     def _():
@@ -534,23 +563,33 @@
             ready, inc=1, device_id={"zero": z.partner}, device_id_type=MESH
         )
         for c, d in rest:
-            stack.forward_y(c, kept(1, c)).start()
-            stack.forward_x(d, kept(2, d)).start()
+            stack.forward_y(c, kept(1, c, 1)).start()
+            stack.forward_x(d, kept(2, d, 1)).start()
         for slot, owner in enumerate(owners):
-            for c in range(count):
-                stack.share(slot, owner, c, kept(slot, c)).start()
-        passed = [c for pair in done for c in pair]
-        for c in passed:
-            stack.share(3, z.across, c, landed.at[2, pl.ds(c * step, step)]).start()
-        moves = [move(slot) for slot in range(3)] + [move_passed(c) for c in passed]
-        for dma in moves:
-            dma.start()
-        for dma in moves:
-            dma.wait()
+            stack.share(slot, owner, 0, count, kept(slot, 0, count)).start()
+        for slot in range(3):
+            move(slot).start()
+        for pair in stack.pairs[:passed]:
+            for c in pair:
+                src = landed.at[2, pl.ds(c * step, step)]
+                stack.share(3, z.across, c, 1, src).start()
+                pltpu.make_async_copy(src, part(z.across, c, 1), l_sems.at[1]).start()
+        pltpu.make_async_copy(whole(3), whole(3), l_sems.at[0]).wait()
+        if passed:
+            moved = part(me, 0, 2 * passed)
+            pltpu.make_async_copy(moved, moved, l_sems.at[1]).wait()
 
     for c, d in rest[:-1]:
         arrive(c, d)
-    sent(rest)
+
+    @pl.when(z.core == 0)
+    def _():
+        stack.wait_forwards()
+
+    @pl.when(z.core == 1)
+    def _():
+        stack.wait_forwards(passed)
+
     if ahead is not None:
         @pl.when(z.core == 0)
         def _():
@@ -566,8 +605,7 @@
         arrive(c, d)
     for slot, owner in enumerate((*owners, z.across)):
         stack.shared(slot, z.other_core(owner))
-        for c in range(count):
-            stack.share(slot, owner, c).wait_send()
+    stack.wait_shares()
     if ahead is not None:
         @pl.when(z.core == 1)
         def _():
@@ -595,7 +633,7 @@
         out_specs=[VMEM] * len(outs),
         scratch_shapes=[
             pltpu.SemaphoreType.REGULAR, pltpu.SemaphoreType.REGULAR,
-            pltpu.SemaphoreType.DMA((3 + COUNTS[s],)),
+            pltpu.SemaphoreType.DMA((2,)),
             *Stack.sems(COUNTS[s]), *ahead,
         ],
         compiler_params=pltpu.CompilerParams(
@@ -629,11 +667,13 @@
         down, gains = refs.pop(0), refs.pop(0)
     del refs[:started]
     outs = {name: refs.pop(0) for name in targets}
-    copies = []
-
-    def go(src, dst):
-        copies.append(pltpu.make_async_copy(src, dst, refs[-1].at[len(copies)]))
-        copies[-1].start()
+    sems = refs[-1]
+
+    def go(src, dst, k):
+        pltpu.make_async_copy(src, dst, sems.at[k]).start()
+
+    def wait(ref, k):
+        pltpu.make_async_copy(ref, ref, sems.at[k]).wait()
 
     token = refs.pop(0) if follows else None
     if norm_of:
@@ -641,20 +681,23 @@
         quarter = down.shape[0] // 4
         for k in range(4):
             at = pl.ds(k * quarter, quarter)
-            go(down.at[at], down_out.at[at])
+            go(down.at[at], down_out.at[at], 1)
     for owner in range(GROUP):
         for name, src, dst, count in pieces:
             go(
                 block.at[owner, pl.ds(src, count)],
                 outs[name].at[pl.ds(owner * rows + dst, count)],
+                0,
             )
     if norm_of:
         lay_norm(*norm_of, gains, lines, laid)
-        go(laid, norm)
+        go(laid, norm, 2)
     if follows:
         token[...] = jnp.zeros_like(token)
-    for copy in copies:
-        copy.wait()
+    if norm_of:
+        wait(laid, 2)
+        wait(down, 1)
+    wait(block, 0)
 
 
 def store(s, block, rows, made, down=None, gains=None, tp=None, size=None):
@@ -680,7 +723,6 @@
             aliases[len(operands)] = k
             operands.append(made[name])
             in_specs.append(ANY)
-    copies = GROUP * len(pieces)
     scratch = []
     if down is not None:
         lines = (GROUP * tp * size // LANES, LANES)
@@ -688,7 +730,6 @@
                  jax.ShapeDtypeStruct(lines, jnp.bfloat16)]
         out_specs += [ANY, ANY]
         scratch += [pltpu.VMEM(lines, jnp.float32), pltpu.VMEM(lines, jnp.bfloat16)]
-        copies += 5
         names += ["down", "norm"]
     results = pl.pallas_call(
         functools.partial(
@@ -698,7 +739,7 @@
         out_shape=tuple(outs),
         in_specs=in_specs,
         out_specs=out_specs,
-        scratch_shapes=[*scratch, pltpu.SemaphoreType.DMA((copies,))],
+        scratch_shapes=[*scratch, pltpu.SemaphoreType.DMA((3 if tp else 1,))],
         input_output_aliases=aliases,
         compiler_params=pltpu.CompilerParams(vmem_limit_bytes=2**20),
         name=f"store_{s}",

time: 162 us -> 161 us (level)
    pallas_call x1, Pallas kernels: 100 us -> 98.2 us  [first(): pl.pallas_call(functools.partial(first_kernel, tp), out_shape=(pltpu.VMEM...]
where the time goes in v3:
time: 161 us
  Pallas kernels  161 us (100%)
    pallas_call x1, Pallas kernels, first(): pl.pallas_call(functools.partial(first_kernel, tp), out_shape=(pltpu.VMEM...  98.2 us
    pallas_call x2, Pallas kernels, later(): pl.pallas_call(functools.partial(later_kernel, s), out_shape=tuple(outs),...  48.7 us
    pallas_call x3, Pallas kernels, store(): pl.pallas_call(functools.partial(store_kernel, pieces, rows, targets, len...  13.7 us

profile of v3, /device:TPU:0, one launch (start us, length us, event | category | flops | bytes accessed | tf_op | source)
XLA Modules:
  0.0 161.2 jit_solution(11996538887592453776)
XLA Ops:
  0.6 98.2 %gather_first.1 = (bf16[8,256,2432]{2,1,0:T(8,128)(2,1)S(1)}, bf16[2432,2560]{1,0:T(8,128)(2,1)S(1)}, bf16[256,2432]{1,0:T(8,128)(2,1)S(1)}, bf16[128,2432]{1,0:...) custom-call(bf16[320,2432]{1,0:T(8,128)(2,1)} %bitcast.7, bf16[16,320]{1,0:T(8,128)(2,1)} %refs_1_.1, ...), custom_call_target="tpu_custom_call" | custom-call | tf_op jit(solution)/shard_map/gather_first/pallas_call | solution.py:451
  98.8 7.6 %store_0.1 = (bf16[2560,2432]{1,0:T(8,128)(2,1)}, f32[8,128]{1,0:T(8,128)S(1)}, bf16[2432,2560]{1,0:T(8,128)(2,1)}, bf16[20,128]{1,0:T(8,128)(2,1)}) custom-call(bf16[8,256,2432]{2,1,0:T(8,128)(2,1)S(1)} %get-tuple-element.21.refs_0_, bf16[2432,2560]{1,0:T(8,128)(2,1)S(1)} %get-tuple-element.22.refs_1_, f32[32,1,128]{2,1,0:T(1,128)S(1)} %get-tuple-element.23.refs_2_), custom_call_target="tpu_custom_call" | custom-call | tf_op jit(solution)/shard_map/store_0/pallas_call | solution.py:734
  106.5 32.0 %gather_1.1 = (bf16[8,256,2432]{2,1,0:T(8,128)(2,1)S(1)}, bf16[3,128,2432]{2,1,0:T(8,128)(2,1)S(1)}) custom-call(bf16[256,2432]{1,0:T(8,128)(2,1)S(1)} %get-tuple-element.19.refs_0_, bf16[3,256,2432]{2,1,0:T(8,128)(2,1)S(1)} %get-tuple-element.20.refs_1_, f32[8,128]{1,0:T(8,128)S(1)} %get-tuple-element.24.refs_2_, ...), custom_call_target="tpu_custom_call" | custom-call | tf_op jit(solution)/shard_map/gather_1/pallas_call | solution.py:629
  138.5 3.8 %store_1.1 = (bf16[2560,2432]{1,0:T(8,128)(2,1)}, bf16[2560,2432]{1,0:T(8,128)(2,1)}, f32[8,128]{1,0:T(8,128)S(1)}) custom-call(bf16[8,256,2432]{2,1,0:T(8,128)(2,1)S(1)} %get-tuple-element.26.refs_0_, bf16[2560,2432]{1,0:T(8,128)(2,1)} %get-tuple-element.27.refs_1_), custom_call_target="tpu_custom_call", output_to_operand_aliasing={{0}: (1, {})} | custom-call | tf_op jit(solution)/shard_map/store_1/pallas_call | solution.py:734
  142.3 16.7 %gather_2.1.refs_0_ = bf16[8,128,2432]{2,1,0:T(8,128)(2,1)S(1)} custom-call(bf16[128,2432]{1,0:T(8,128)(2,1)S(1)} %get-tuple-element.25.refs_3_.refs_0_, bf16[3,128,2432]{2,1,0:T(8,128)(2,1)S(1)} %get-tuple-element.29.refs_1_, f32[8,128]{1,0:T(8,128)S(1)} %get-tuple-element.30.refs_2_), custom_call_target="tpu_custom_call" | custom-call | tf_op jit(solution)/shard_map/gather_2/pallas_call | solution.py:629
  159.0 2.3 %store_2.1 = bf16[2560,2432]{1,0:T(8,128)(2,1)} custom-call(bf16[8,128,2432]{2,1,0:T(8,128)(2,1)S(1)} %gather_2.1.refs_0_, bf16[2560,2432]{1,0:T(8,128)(2,1)} %get-tuple-element.31.refs_1_), custom_call_target="tpu_custom_call", output_to_operand_aliasing={{}: (1, {})} | custom-call | tf_op jit(solution)/shard_map/store_2/pallas_call | solution.py:734
